TPU v7x, 32 devices: a whole 2x2x4 slice. The times are simulated.
32 devices in a mesh: srow: 4 (over y, core), scol: 8 (over z, x).
Axes of the slice: x: 2, y: 2, z: 4, core: 2. Of those that a mesh axis runs over, the one named last changes fastest.
Arguments:
- loads: float32 [4, 16, 4, 128], P('srow', 'scol'), may hold values from -6 to 6
- local_inverse: float32 [4, 16, 128, 128], P('srow', 'scol'), as said below
- dirichlet: float32 [4, 16, 128, 128], P('srow', 'scol'), as said below
- corner_coupling: float32 [4, 16, 128], P('srow', 'scol'), may hold values from -4 to 4
- coarse_inverse: float32 [4, 16, 16], P('srow', 'scol'), as said below
- partner: int32 [4, 16, 128], P('srow', 'scol'), may hold values from -1 to 31, as said below
Outputs:
- multipliers: float32 [4, 16, 4, 128], P('srow', 'scol')
- residual: float32 [4, 16, 4, 128], P('srow', 'scol')
Inputs may be any that keep to these rules, and one draw needn't show every extreme that they name: `partner`: on each edge of each subdomain the first n entries, for some n of 1 to 32, are the positions 0 to n - 1 in order or reversed, the rest are -1; the two subdomains sharing an edge have the same n and mutually inverse lists. `local_inverse`: each block is symmetric positive definite. `dirichlet`: each block is symmetric positive definite. `coarse_inverse`: each band's matrix is symmetric positive definite.
All inputs are finite; a program needn't handle non-finite values.
Results may differ from a plain program's by a relative error of at most 0.0003.
Values sent between devices are 32-bit elements; how exact they have to be, the bound alone decides.
A program may use at most 64 MiB of HBM per device.

v0:
```python
import jax
import jax.numpy as jnp
from jax import lax
from jax.sharding import PartitionSpec as P

ITERS = 3
precise = lax.Precision.HIGHEST


def with_halo(cells, sides, width):
    for axis, dim in sides:
        count = lax.axis_size(axis)
        head = lax.slice_in_dim(cells, 0, width, axis=dim)
        tail = lax.slice_in_dim(cells, cells.shape[dim] - width, cells.shape[dim], axis=dim)
        cells = jnp.concatenate(
            [
                lax.ppermute(tail, axis, [(i, (i + 1) % count) for i in range(count)]),
                cells,
                lax.ppermute(head, axis, [((i + 1) % count, i) for i in range(count)]),
            ],
            axis=dim,
        )
    return cells


def facing_edges(values):
    edge_len = values.shape[-1] // 4
    sideways = with_halo(values[..., 0 : 2 * edge_len], (("scol", 1),), 1)
    vertical = with_halo(values[..., 2 * edge_len :], (("srow", 0),), 1)
    west_side = sideways[:, :-2, :, edge_len : 2 * edge_len]
    east_side = sideways[:, 2:, :, 0:edge_len]
    south_side = vertical[:-2, :, :, edge_len : 2 * edge_len]
    north_side = vertical[2:, :, :, 0:edge_len]
    return jnp.concatenate([west_side, east_side, south_side, north_side], axis=-1)


def jump(values, partner):
    edge_len = values.shape[-1] // 4
    facing = facing_edges(values)
    offset = jnp.arange(values.shape[-1], dtype=jnp.int32) // edge_len * edge_len
    position = jnp.clip(partner, 0, edge_len - 1) + offset
    position = jnp.broadcast_to(position[:, :, None, :], values.shape)
    picked = jnp.take_along_axis(facing, position, axis=-1)
    return jnp.where(partner[:, :, None, :] >= 0, values - picked, jnp.zeros_like(values))


def apply_inverse(values, local_inverse, corner_coupling, coarse_inverse):
    sub_rows, sub_cols, rhs_count, width = values.shape
    blocks = jnp.einsum("ijab,ijrb->ijra", local_inverse, values, precision=precise)
    coarse_in = jnp.einsum("ijb,ijrb->ijr", corner_coupling, values, precision=precise)
    coarse_in = coarse_in.reshape(sub_rows * sub_cols, rhs_count)
    band_rows = coarse_inverse[0]
    coarse_out = jnp.dot(
        band_rows,
        lax.all_gather(coarse_in, "scol", axis=0, tiled=True),
        precision=precise,
        preferred_element_type=jnp.float32,
    )
    coarse_out = coarse_out.reshape(sub_rows, sub_cols, rhs_count)
    return blocks + corner_coupling[:, :, None, :] * coarse_out[..., None]


def inner(left, right):
    return jnp.sum(left * right, axis=(0, 1, 3))


def global_sums(first_dot, second_dot):
    return lax.psum((first_dot, second_dot), ("srow", "scol"))


def scaled(coef, values):
    return coef[None, None, :, None] * values


def body(loads, local_inverse, dirichlet, corner_coupling, coarse_inverse, partner):

    def operator(values):
        spread = jump(values, partner)
        return jump(apply_inverse(spread, local_inverse, corner_coupling, coarse_inverse), partner)

    def precond(values):
        spread = jump(values, partner)
        return jump(jnp.einsum("ijab,ijrb->ijra", dirichlet, spread, precision=precise), partner)

    right = operator(loads)
    multipliers = jnp.zeros_like(right)
    residual = right
    precon = precond(residual)
    image = operator(precon)
    gamma, curvature = global_sums(inner(residual, precon), inner(precon, image))
    step_size = gamma / curvature
    search = precon
    along = image
    for iteration in range(ITERS):
        multipliers = multipliers + scaled(step_size, search)
        residual = residual - scaled(step_size, along)
        if iteration + 1 < ITERS:
            precon = precond(residual)
            image = operator(precon)
            gamma_new, curvature = global_sums(inner(residual, precon), inner(precon, image))
            dir_ratio = gamma_new / gamma
            step_size = gamma_new / (curvature - dir_ratio * gamma_new / step_size)
            search = precon + scaled(dir_ratio, search)
            along = image + scaled(dir_ratio, along)
            gamma = gamma_new
    return (multipliers, residual)


def solution(mesh):
    return jax.shard_map(
        body,
        mesh=mesh,
        in_specs=(
            P("srow", "scol", None, None),
            P("srow", "scol", None, None),
            P("srow", "scol", None, None),
            P("srow", "scol", None),
            P("srow", "scol", None),
            P("srow", "scol", None),
        ),
        out_specs=(P("srow", "scol", None, None), P("srow", "scol", None, None)),
        check_vma=False,
    )
```

profile of v0, /device:TPU:0, one launch (start us, length us, event | category | flops | bytes accessed | tf_op | source)
XLA Modules:
  0.0 464.1 jit_solution(16173901481340105120)
XLA Ops:
  2.0 1.9 collective-permute-start.3
  4.0 2.3 collective-permute-start
  6.2 3.1 collective-permute-start.1
  10.9 9.6 %gather_fusion = f32[1024]{0:T(1024)S(1)} fusion(f32[2,4,128]{2,1,0:T(4,128)S(1)} %fusion.69, s32[1024]{0:T(1024)S(1)} %bitcast.196), kind=kCustom, calls=%fused_computation.clone | custom fusion | bytes 20480 | tf_op jit(solution)/shard_map/jit(take_along_axis)/gather | solution.py:43
  21.3 21.1 %all-gather = f32[8,2,4]{2,1,0:T(2,128)S(1)} all-gather(f32[1,2,4]{2,1,0:T(2,128)S(1)} %bitcast.256), channel_id=1, replica_groups=mesh['srow'=4,'scol'=8] {'scol'}, dimensions={0}, use_global_device_ids=true | all-gather | bytes 288 | tf_op jit(solution)/shard_map/all_gather | solution.py:55
  43.6 1.7 collective-permute-start.7
  45.4 4.7 %collective-permute-start.5 = (f32[1,1,4,64]{3,2,1,0:T(4,128)S(1)}, f32[1,1,4,64]{3,2,1,0:T(4,128)S(1)}, u32[]{:S(2)}, u32[]{:S(2)}) collective-permute-start(f32[1,1,4,64]{3,2,1,0:T(4,128)S(1)} %get-tuple-element.76), channel_id=1, source_target_pairs={{1,0},{2,1},{3,2},{4,3},{5,4},{6,5},{7,6},{0,7},{9,8},{10,9},{11,1... | collective-permute-start | bytes 3080 | tf_op jit(solution)/shard_map/ppermute | solution.py:19
  50.2 1.5 collective-permute-done.4
  51.7 9.6 %gather_fusion.1 = f32[1024]{0:T(1024)S(1)} fusion(f32[2,4,128]{2,1,0:T(4,128)S(1)} %fusion.65, s32[1024]{0:T(1024)S(1)} %bitcast.197), kind=kCustom, calls=%fused_computation.1.clone | custom fusion | bytes 20480 | tf_op jit(solution)/shard_map/jit(take_along_axis)/gather | solution.py:43
  61.5 1.7 collective-permute-start.11
  63.2 4.7 %collective-permute-start.9 = (f32[1,1,4,64]{3,2,1,0:T(4,128)S(1)}, f32[1,1,4,64]{3,2,1,0:T(4,128)S(1)}, u32[]{:S(2)}, u32[]{:S(2)}) collective-permute-start(f32[1,1,4,64]{3,2,1,0:T(4,128)S(1)} %get-tuple-element.72), channel_id=1, source_target_pairs={{1,0},{2,1},{3,2},{4,3},{5,4},{6,5},{7,6},{0,7},{9,8},{10,9},{11,1... | collective-permute-start | bytes 3080 | tf_op jit(solution)/shard_map/ppermute | solution.py:19
  68.0 1.5 collective-permute-done.8
  69.6 9.6 %gather_fusion.2 = f32[1024]{0:T(1024)S(1)} fusion(f32[2,4,128]{2,1,0:T(4,128)S(1)} %fusion.61, s32[1024]{0:T(1024)S(1)} %bitcast.198), kind=kCustom, calls=%fused_computation.2.clone | custom fusion | bytes 20480 | tf_op jit(solution)/shard_map/jit(take_along_axis)/gather | solution.py:43
  79.6 1.8 collective-permute-start.15
  81.3 4.7 %collective-permute-start.13 = (f32[1,1,4,64]{3,2,1,0:T(4,128)S(1)}, f32[1,1,4,64]{3,2,1,0:T(4,128)S(1)}, u32[]{:S(2)}, u32[]{:S(2)}) collective-permute-start(f32[1,1,4,64]{3,2,1,0:T(4,128)S(1)} %get-tuple-element.68), channel_id=1, source_target_pairs={{1,0},{2,1},{3,2},{4,3},{5,4},{6,5},{7,6},{0,7},{9,8},{10,9},{11,1... | collective-permute-start | bytes 3080 | tf_op jit(solution)/shard_map/ppermute | solution.py:19
  86.1 1.5 collective-permute-done.12
  87.7 9.6 %gather_fusion.3 = f32[1024]{0:T(1024)S(1)} fusion(f32[2,4,128]{2,1,0:T(4,128)S(1)} %fusion.57, s32[1024]{0:T(1024)S(1)} %bitcast.199), kind=kCustom, calls=%fused_computation.3.clone | custom fusion | bytes 20480 | tf_op jit(solution)/shard_map/jit(take_along_axis)/gather | solution.py:43
  97.4 1.7 collective-permute-start.19
  99.2 4.7 %collective-permute-start.17 = (f32[1,1,4,64]{3,2,1,0:T(4,128)S(1)}, f32[1,1,4,64]{3,2,1,0:T(4,128)S(1)}, u32[]{:S(2)}, u32[]{:S(2)}) collective-permute-start(f32[1,1,4,64]{3,2,1,0:T(4,128)S(1)} %get-tuple-element.64), channel_id=1, source_target_pairs={{1,0},{2,1},{3,2},{4,3},{5,4},{6,5},{7,6},{0,7},{9,8},{10,9},{11,1... | collective-permute-start | bytes 3080 | tf_op jit(solution)/shard_map/ppermute | solution.py:19
  104.0 1.5 collective-permute-done.16
  105.5 9.6 %gather_fusion.4 = f32[1024]{0:T(1024)S(1)} fusion(f32[2,4,128]{2,1,0:T(4,128)S(1)} %fusion.53, s32[1024]{0:T(1024)S(1)} %bitcast.200), kind=kCustom, calls=%fused_computation.4.clone | custom fusion | bytes 20480 | tf_op jit(solution)/shard_map/jit(take_along_axis)/gather | solution.py:43
  115.3 21.0 %all-gather.1 = f32[8,2,4]{2,1,0:T(2,128)S(1)} all-gather(f32[1,2,4]{2,1,0:T(2,128)S(1)} %bitcast.257), channel_id=1, replica_groups=mesh['srow'=4,'scol'=8] {'scol'}, dimensions={0}, use_global_device_ids=true | all-gather | bytes 288 | tf_op jit(solution)/shard_map/all_gather | solution.py:55
  136.8 1.7 collective-permute-start.23
  138.6 4.7 %collective-permute-start.21 = (f32[1,1,4,64]{3,2,1,0:T(4,128)S(1)}, f32[1,1,4,64]{3,2,1,0:T(4,128)S(1)}, u32[]{:S(2)}, u32[]{:S(2)}) collective-permute-start(f32[1,1,4,64]{3,2,1,0:T(4,128)S(1)} %get-tuple-element.60), channel_id=1, source_target_pairs={{1,0},{2,1},{3,2},{4,3},{5,4},{6,5},{7,6},{0,7},{9,8},{10,9},{11,1... | collective-permute-start | bytes 3080 | tf_op jit(solution)/shard_map/ppermute | solution.py:19
  143.4 1.5 collective-permute-done.20
  144.9 9.6 %gather_fusion.5 = f32[1024]{0:T(1024)S(1)} fusion(f32[2,4,128]{2,1,0:T(4,128)S(1)} %fusion.49, s32[1024]{0:T(1024)S(1)} %bitcast.201), kind=kCustom, calls=%fused_computation.5.clone | custom fusion | bytes 20480 | tf_op jit(solution)/shard_map/jit(take_along_axis)/gather | solution.py:43
  154.7 40.2 %all-reduce.2 = (f32[4]{0:T(128)S(1)}, f32[4]{0:T(128)S(1)}) all-reduce(f32[4]{0:T(128)S(1)} %get-tuple-element.8, f32[4]{0:T(128)S(1)} %get-tuple-element.7), channel_id=1, replica_groups=mesh['srow'=4,'scol'=8] {'srow','scol'}, use_global_device_ids=true, to_apply=%region_1.3 | all-reduce | flops 8 | bytes 64 | tf_op jit(solution)/shard_map/psum | solution.py:68
  195.1 1.7 collective-permute-start.27
  196.8 2.3 collective-permute-start.24
  199.1 2.4 collective-permute-start.25
  201.6 1.5 collective-permute-done.24
  203.2 9.6 %gather_fusion.6 = f32[1024]{0:T(1024)S(1)} fusion(f32[2,4,128]{2,1,0:T(4,128)S(1)} %fusion.45, s32[1024]{0:T(1024)S(1)} %bitcast.202), kind=kCustom, calls=%fused_computation.6.clone | custom fusion | bytes 20480 | tf_op jit(solution)/shard_map/jit(take_along_axis)/gather | solution.py:43
  213.2 1.8 collective-permute-start.31
  214.9 1.8 collective-permute-start.28
  216.7 2.9 collective-permute-start.29
  219.7 1.5 collective-permute-done.28
  221.3 9.6 %gather_fusion.7 = f32[1024]{0:T(1024)S(1)} fusion(f32[2,4,128]{2,1,0:T(4,128)S(1)} %fusion.41, s32[1024]{0:T(1024)S(1)} %bitcast.203), kind=kCustom, calls=%fused_computation.7.clone | custom fusion | bytes 20480 | tf_op jit(solution)/shard_map/jit(take_along_axis)/gather | solution.py:43
  231.0 1.7 collective-permute-start.35
  234.1 3.4 collective-permute-start.33
  237.6 1.5 collective-permute-done.32
  239.1 9.6 %gather_fusion.8 = f32[1024]{0:T(1024)S(1)} fusion(f32[2,4,128]{2,1,0:T(4,128)S(1)} %fusion.37, s32[1024]{0:T(1024)S(1)} %bitcast.204), kind=kCustom, calls=%fused_computation.8.clone | custom fusion | bytes 20480 | tf_op jit(solution)/shard_map/jit(take_along_axis)/gather | solution.py:43
  248.9 21.0 %all-gather.2 = f32[8,2,4]{2,1,0:T(2,128)S(1)} all-gather(f32[1,2,4]{2,1,0:T(2,128)S(1)} %bitcast.258), channel_id=1, replica_groups=mesh['srow'=4,'scol'=8] {'scol'}, dimensions={0}, use_global_device_ids=true | all-gather | bytes 288 | tf_op jit(solution)/shard_map/all_gather | solution.py:55
  270.4 1.7 collective-permute-start.39
  272.2 4.7 %collective-permute-start.37 = (f32[1,1,4,64]{3,2,1,0:T(4,128)S(1)}, f32[1,1,4,64]{3,2,1,0:T(4,128)S(1)}, u32[]{:S(2)}, u32[]{:S(2)}) collective-permute-start(f32[1,1,4,64]{3,2,1,0:T(4,128)S(1)} %get-tuple-element.44), channel_id=1, source_target_pairs={{1,0},{2,1},{3,2},{4,3},{5,4},{6,5},{7,6},{0,7},{9,8},{10,9},{11,1... | collective-permute-start | bytes 3080 | tf_op jit(solution)/shard_map/ppermute | solution.py:19
  278.5 9.6 %gather_fusion.9 = f32[1024]{0:T(1024)S(1)} fusion(f32[2,4,128]{2,1,0:T(4,128)S(1)} %fusion.33, s32[1024]{0:T(1024)S(1)} %bitcast.205), kind=kCustom, calls=%fused_computation.9.clone | custom fusion | bytes 20480 | tf_op jit(solution)/shard_map/jit(take_along_axis)/gather | solution.py:43
  288.3 40.8 %all-reduce.1 = (f32[4]{0:T(128)S(1)}, f32[4]{0:T(128)S(1)}) all-reduce(f32[4]{0:T(128)S(1)} %get-tuple-element.6, f32[4]{0:T(128)S(1)} %get-tuple-element.5), channel_id=1, replica_groups=mesh['srow'=4,'scol'=8] {'srow','scol'}, use_global_device_ids=true, to_apply=%region_5.7 | all-reduce | flops 8 | bytes 64 | tf_op jit(solution)/shard_map/psum | solution.py:68
  329.3 1.8 collective-permute-start.43
  331.1 2.3 collective-permute-start.40
  333.3 2.4 collective-permute-start.41
  337.4 9.6 %gather_fusion.10 = f32[1024]{0:T(1024)S(1)} fusion(f32[2,4,128]{2,1,0:T(4,128)S(1)} %fusion.29, s32[1024]{0:T(1024)S(1)} %bitcast.206), kind=kCustom, calls=%fused_computation.10.clone | custom fusion | bytes 20480 | tf_op jit(solution)/shard_map/jit(take_along_axis)/gather | solution.py:43
  347.4 1.8 collective-permute-start.47
  349.2 1.8 collective-permute-start.44
  351.0 2.9 collective-permute-start.45
  354.0 1.5 collective-permute-done.44
  355.5 9.6 %gather_fusion.11 = f32[1024]{0:T(1024)S(1)} fusion(f32[2,4,128]{2,1,0:T(4,128)S(1)} %fusion.25, s32[1024]{0:T(1024)S(1)} %bitcast.207), kind=kCustom, calls=%fused_computation.11.clone | custom fusion | bytes 20480 | tf_op jit(solution)/shard_map/jit(take_along_axis)/gather | solution.py:43
  365.3 1.7 collective-permute-start.51
  368.4 3.4 collective-permute-start.49
  371.8 1.5 collective-permute-done.48
  373.4 9.6 %gather_fusion.12 = f32[1024]{0:T(1024)S(1)} fusion(f32[2,4,128]{2,1,0:T(4,128)S(1)} %fusion.21, s32[1024]{0:T(1024)S(1)} %bitcast.208), kind=kCustom, calls=%fused_computation.12.clone | custom fusion | bytes 20480 | tf_op jit(solution)/shard_map/jit(take_along_axis)/gather | solution.py:43
  383.1 21.0 %all-gather.3 = f32[8,2,4]{2,1,0:T(2,128)S(1)} all-gather(f32[1,2,4]{2,1,0:T(2,128)S(1)} %bitcast.259), channel_id=1, replica_groups=mesh['srow'=4,'scol'=8] {'scol'}, dimensions={0}, use_global_device_ids=true | all-gather | bytes 288 | tf_op jit(solution)/shard_map/all_gather | solution.py:55
  404.7 1.7 collective-permute-start.55
  406.4 4.7 %collective-permute-start.53 = (f32[1,1,4,64]{3,2,1,0:T(4,128)S(1)}, f32[1,1,4,64]{3,2,1,0:T(4,128)S(1)}, u32[]{:S(2)}, u32[]{:S(2)}) collective-permute-start(f32[1,1,4,64]{3,2,1,0:T(4,128)S(1)} %get-tuple-element.28), channel_id=1, source_target_pairs={{1,0},{2,1},{3,2},{4,3},{5,4},{6,5},{7,6},{0,7},{9,8},{10,9},{11,1... | collective-permute-start | bytes 3080 | tf_op jit(solution)/shard_map/ppermute | solution.py:19
  412.8 9.6 %gather_fusion.13 = f32[1024]{0:T(1024)S(1)} fusion(f32[2,4,128]{2,1,0:T(4,128)S(1)} %fusion.17, s32[1024]{0:T(1024)S(1)} %bitcast.209), kind=kCustom, calls=%fused_computation.13.clone | custom fusion | bytes 20480 | tf_op jit(solution)/shard_map/jit(take_along_axis)/gather | solution.py:43
  422.5 40.8 %all-reduce = (f32[4]{0:T(128)S(1)}, f32[4]{0:T(128)S(1)}) all-reduce(f32[4]{0:T(128)S(1)} %get-tuple-element.4, f32[4]{0:T(128)S(1)} %get-tuple-element.3), channel_id=1, replica_groups=mesh['srow'=4,'scol'=8] {'srow','scol'}, use_global_device_ids=true, to_apply=%region_9.11 | all-reduce | flops 8 | bytes 64 | tf_op jit(solution)/shard_map/psum | solution.py:68
  (171 shorter events, 19.1 us)
Async XLA Ops:
  0.6 42.6 %copy-start = (f32[1,2,128,128]{3,2,1,0:T(8,128)S(1)}, f32[1,2,128,128]{3,2,1,0:T(8,128)}, u32[]{:S(2)}) copy-start(f32[1,2,128,128]{3,2,1,0:T(8,128)} %param.9) | copy-start | bytes 393220
  0.6 3.3 copy-start.2
  1.5 7.9 %collective-permute-start.2 = (f32[1,2,4,64]{3,2,1,0:T(4,128)S(1)}, f32[1,2,4,64]{3,2,1,0:T(4,128)S(1)}, u32[]{:S(2)}, u32[]{:S(2)}) collective-permute-start(f32[1,2,4,64]{3,2,1,0:T(4,128)S(1)} %get-tuple-element.77), channel_id=1, source_target_pairs={{0,8},{8,16},{16,24},{24,0},{1,9},{9,17},{17,25},{25,1},{2,10},{10... | collective-permute-start | bytes 6152 | tf_op jit(solution)/shard_map/ppermute | solution.py:17
  2.0 8.8 %collective-permute-start.3 = (f32[1,2,4,64]{3,2,1,0:T(4,128)S(1)}, f32[1,2,4,64]{3,2,1,0:T(4,128)S(1)}, u32[]{:S(2)}, u32[]{:S(2)}) collective-permute-start(f32[1,2,4,64]{3,2,1,0:T(4,128)S(1)} %get-tuple-element.77), channel_id=1, source_target_pairs={{8,0},{16,8},{24,16},{0,24},{9,1},{17,9},{25,17},{1,25},{10,2},{18... | collective-permute-start | bytes 6152 | tf_op jit(solution)/shard_map/ppermute | solution.py:19
  4.0 6.9 %collective-permute-start = (f32[1,1,4,64]{3,2,1,0:T(4,128)S(1)}, f32[1,1,4,64]{3,2,1,0:T(4,128)S(1)}, u32[]{:S(2)}, u32[]{:S(2)}) collective-permute-start(f32[1,1,4,64]{3,2,1,0:T(4,128)S(1)} %get-tuple-element.79), channel_id=1, source_target_pairs={{0,1},{1,2},{2,3},{3,4},{4,5},{5,6},{6,7},{7,0},{8,9},{9,10},{10,1... | collective-permute-start | bytes 3080 | tf_op jit(solution)/shard_map/ppermute | solution.py:17
  6.2 3.1 copy-start.5
  6.2 4.6 collective-permute-start.1
  20.5 0.7 copy-start.3
  42.4 0.7 copy-start.4
  43.6 6.5 %collective-permute-start.6 = (f32[1,2,4,64]{3,2,1,0:T(4,128)S(1)}, f32[1,2,4,64]{3,2,1,0:T(4,128)S(1)}, u32[]{:S(2)}, u32[]{:S(2)}) collective-permute-start(f32[1,2,4,64]{3,2,1,0:T(4,128)S(1)} %get-tuple-element.73), channel_id=1, source_target_pairs={{0,8},{8,16},{16,24},{24,0},{1,9},{9,17},{17,25},{25,1},{2,10},{10... | collective-permute-start | bytes 6152 | tf_op jit(solution)/shard_map/ppermute | solution.py:17
  43.6 8.0 %collective-permute-start.7 = (f32[1,2,4,64]{3,2,1,0:T(4,128)S(1)}, f32[1,2,4,64]{3,2,1,0:T(4,128)S(1)}, u32[]{:S(2)}, u32[]{:S(2)}) collective-permute-start(f32[1,2,4,64]{3,2,1,0:T(4,128)S(1)} %get-tuple-element.73), channel_id=1, source_target_pairs={{8,0},{16,8},{24,16},{0,24},{9,1},{17,9},{25,17},{1,25},{10,2},{18... | collective-permute-start | bytes 6152 | tf_op jit(solution)/shard_map/ppermute | solution.py:19
  45.4 6.3 %collective-permute-start.4 = (f32[1,1,4,64]{3,2,1,0:T(4,128)S(1)}, f32[1,1,4,64]{3,2,1,0:T(4,128)S(1)}, u32[]{:S(2)}, u32[]{:S(2)}) collective-permute-start(f32[1,1,4,64]{3,2,1,0:T(4,128)S(1)} %get-tuple-element.75), channel_id=1, source_target_pairs={{0,1},{1,2},{2,3},{3,4},{4,5},{5,6},{6,7},{7,0},{8,9},{9,10},{10,1... | collective-permute-start | bytes 3080 | tf_op jit(solution)/shard_map/ppermute | solution.py:17
  45.4 6.3 %collective-permute-start.5 = (f32[1,1,4,64]{3,2,1,0:T(4,128)S(1)}, f32[1,1,4,64]{3,2,1,0:T(4,128)S(1)}, u32[]{:S(2)}, u32[]{:S(2)}) collective-permute-start(f32[1,1,4,64]{3,2,1,0:T(4,128)S(1)} %get-tuple-element.76), channel_id=1, source_target_pairs={{1,0},{2,1},{3,2},{4,3},{5,4},{6,5},{7,6},{0,7},{9,8},{10,9},{11,1... | collective-permute-start | bytes 3080 | tf_op jit(solution)/shard_map/ppermute | solution.py:19
  61.4 6.5 %collective-permute-start.10 = (f32[1,2,4,64]{3,2,1,0:T(4,128)S(1)}, f32[1,2,4,64]{3,2,1,0:T(4,128)S(1)}, u32[]{:S(2)}, u32[]{:S(2)}) collective-permute-start(f32[1,2,4,64]{3,2,1,0:T(4,128)S(1)} %get-tuple-element.69), channel_id=1, source_target_pairs={{0,8},{8,16},{16,24},{24,0},{1,9},{9,17},{17,25},{25,1},{2,10},{10... | collective-permute-start | bytes 6152 | tf_op jit(solution)/shard_map/ppermute | solution.py:17
  61.5 8.0 %collective-permute-start.11 = (f32[1,2,4,64]{3,2,1,0:T(4,128)S(1)}, f32[1,2,4,64]{3,2,1,0:T(4,128)S(1)}, u32[]{:S(2)}, u32[]{:S(2)}) collective-permute-start(f32[1,2,4,64]{3,2,1,0:T(4,128)S(1)} %get-tuple-element.69), channel_id=1, source_target_pairs={{8,0},{16,8},{24,16},{0,24},{9,1},{17,9},{25,17},{1,25},{10,2},{18... | collective-permute-start | bytes 6152 | tf_op jit(solution)/shard_map/ppermute | solution.py:19
  63.2 6.3 %collective-permute-start.8 = (f32[1,1,4,64]{3,2,1,0:T(4,128)S(1)}, f32[1,1,4,64]{3,2,1,0:T(4,128)S(1)}, u32[]{:S(2)}, u32[]{:S(2)}) collective-permute-start(f32[1,1,4,64]{3,2,1,0:T(4,128)S(1)} %get-tuple-element.71), channel_id=1, source_target_pairs={{0,1},{1,2},{2,3},{3,4},{4,5},{5,6},{6,7},{7,0},{8,9},{9,10},{10,1... | collective-permute-start | bytes 3080 | tf_op jit(solution)/shard_map/ppermute | solution.py:17
  63.2 6.3 %collective-permute-start.9 = (f32[1,1,4,64]{3,2,1,0:T(4,128)S(1)}, f32[1,1,4,64]{3,2,1,0:T(4,128)S(1)}, u32[]{:S(2)}, u32[]{:S(2)}) collective-permute-start(f32[1,1,4,64]{3,2,1,0:T(4,128)S(1)} %get-tuple-element.72), channel_id=1, source_target_pairs={{1,0},{2,1},{3,2},{4,3},{5,4},{6,5},{7,6},{0,7},{9,8},{10,9},{11,1... | collective-permute-start | bytes 3080 | tf_op jit(solution)/shard_map/ppermute | solution.py:19
  69.6 9.6 %copy-start.1 = (f32[1,2,128,128]{3,2,1,0:T(8,128)S(1)}, f32[1,2,128,128]{3,2,1,0:T(8,128)}, u32[]{:S(2)}) copy-start(f32[1,2,128,128]{3,2,1,0:T(8,128)} %param.10) | copy-start | bytes 393220
  79.6 6.5 %collective-permute-start.14 = (f32[1,2,4,64]{3,2,1,0:T(4,128)S(1)}, f32[1,2,4,64]{3,2,1,0:T(4,128)S(1)}, u32[]{:S(2)}, u32[]{:S(2)}) collective-permute-start(f32[1,2,4,64]{3,2,1,0:T(4,128)S(1)} %get-tuple-element.65), channel_id=1, source_target_pairs={{0,8},{8,16},{16,24},{24,0},{1,9},{9,17},{17,25},{25,1},{2,10},{10... | collective-permute-start | bytes 6152 | tf_op jit(solution)/shard_map/ppermute | solution.py:17
  79.6 8.0 %collective-permute-start.15 = (f32[1,2,4,64]{3,2,1,0:T(4,128)S(1)}, f32[1,2,4,64]{3,2,1,0:T(4,128)S(1)}, u32[]{:S(2)}, u32[]{:S(2)}) collective-permute-start(f32[1,2,4,64]{3,2,1,0:T(4,128)S(1)} %get-tuple-element.65), channel_id=1, source_target_pairs={{8,0},{16,8},{24,16},{0,24},{9,1},{17,9},{25,17},{1,25},{10,2},{18... | collective-permute-start | bytes 6152 | tf_op jit(solution)/shard_map/ppermute | solution.py:19
  81.3 6.3 %collective-permute-start.12 = (f32[1,1,4,64]{3,2,1,0:T(4,128)S(1)}, f32[1,1,4,64]{3,2,1,0:T(4,128)S(1)}, u32[]{:S(2)}, u32[]{:S(2)}) collective-permute-start(f32[1,1,4,64]{3,2,1,0:T(4,128)S(1)} %get-tuple-element.67), channel_id=1, source_target_pairs={{0,1},{1,2},{2,3},{3,4},{4,5},{5,6},{6,7},{7,0},{8,9},{9,10},{10,1... | collective-permute-start | bytes 3080 | tf_op jit(solution)/shard_map/ppermute | solution.py:17
  81.3 6.3 %collective-permute-start.13 = (f32[1,1,4,64]{3,2,1,0:T(4,128)S(1)}, f32[1,1,4,64]{3,2,1,0:T(4,128)S(1)}, u32[]{:S(2)}, u32[]{:S(2)}) collective-permute-start(f32[1,1,4,64]{3,2,1,0:T(4,128)S(1)} %get-tuple-element.68), channel_id=1, source_target_pairs={{1,0},{2,1},{3,2},{4,3},{5,4},{6,5},{7,6},{0,7},{9,8},{10,9},{11,1... | collective-permute-start | bytes 3080 | tf_op jit(solution)/shard_map/ppermute | solution.py:19
  97.4 6.5 %collective-permute-start.18 = (f32[1,2,4,64]{3,2,1,0:T(4,128)S(1)}, f32[1,2,4,64]{3,2,1,0:T(4,128)S(1)}, u32[]{:S(2)}, u32[]{:S(2)}) collective-permute-start(f32[1,2,4,64]{3,2,1,0:T(4,128)S(1)} %get-tuple-element.61), channel_id=1, source_target_pairs={{0,8},{8,16},{16,24},{24,0},{1,9},{9,17},{17,25},{25,1},{2,10},{10... | collective-permute-start | bytes 6152 | tf_op jit(solution)/shard_map/ppermute | solution.py:17
  97.4 8.0 %collective-permute-start.19 = (f32[1,2,4,64]{3,2,1,0:T(4,128)S(1)}, f32[1,2,4,64]{3,2,1,0:T(4,128)S(1)}, u32[]{:S(2)}, u32[]{:S(2)}) collective-permute-start(f32[1,2,4,64]{3,2,1,0:T(4,128)S(1)} %get-tuple-element.61), channel_id=1, source_target_pairs={{8,0},{16,8},{24,16},{0,24},{9,1},{17,9},{25,17},{1,25},{10,2},{18... | collective-permute-start | bytes 6152 | tf_op jit(solution)/shard_map/ppermute | solution.py:19
  99.2 6.3 %collective-permute-start.16 = (f32[1,1,4,64]{3,2,1,0:T(4,128)S(1)}, f32[1,1,4,64]{3,2,1,0:T(4,128)S(1)}, u32[]{:S(2)}, u32[]{:S(2)}) collective-permute-start(f32[1,1,4,64]{3,2,1,0:T(4,128)S(1)} %get-tuple-element.63), channel_id=1, source_target_pairs={{0,1},{1,2},{2,3},{3,4},{4,5},{5,6},{6,7},{7,0},{8,9},{9,10},{10,1... | collective-permute-start | bytes 3080 | tf_op jit(solution)/shard_map/ppermute | solution.py:17
  99.2 6.3 %collective-permute-start.17 = (f32[1,1,4,64]{3,2,1,0:T(4,128)S(1)}, f32[1,1,4,64]{3,2,1,0:T(4,128)S(1)}, u32[]{:S(2)}, u32[]{:S(2)}) collective-permute-start(f32[1,1,4,64]{3,2,1,0:T(4,128)S(1)} %get-tuple-element.64), channel_id=1, source_target_pairs={{1,0},{2,1},{3,2},{4,3},{5,4},{6,5},{7,6},{0,7},{9,8},{10,9},{11,1... | collective-permute-start | bytes 3080 | tf_op jit(solution)/shard_map/ppermute | solution.py:19
  136.8 6.5 %collective-permute-start.22 = (f32[1,2,4,64]{3,2,1,0:T(4,128)S(1)}, f32[1,2,4,64]{3,2,1,0:T(4,128)S(1)}, u32[]{:S(2)}, u32[]{:S(2)}) collective-permute-start(f32[1,2,4,64]{3,2,1,0:T(4,128)S(1)} %get-tuple-element.57), channel_id=1, source_target_pairs={{0,8},{8,16},{16,24},{24,0},{1,9},{9,17},{17,25},{25,1},{2,10},{10... | collective-permute-start | bytes 6152 | tf_op jit(solution)/shard_map/ppermute | solution.py:17
  136.8 8.0 %collective-permute-start.23 = (f32[1,2,4,64]{3,2,1,0:T(4,128)S(1)}, f32[1,2,4,64]{3,2,1,0:T(4,128)S(1)}, u32[]{:S(2)}, u32[]{:S(2)}) collective-permute-start(f32[1,2,4,64]{3,2,1,0:T(4,128)S(1)} %get-tuple-element.57), channel_id=1, source_target_pairs={{8,0},{16,8},{24,16},{0,24},{9,1},{17,9},{25,17},{1,25},{10,2},{18... | collective-permute-start | bytes 6152 | tf_op jit(solution)/shard_map/ppermute | solution.py:19
  138.6 6.3 %collective-permute-start.20 = (f32[1,1,4,64]{3,2,1,0:T(4,128)S(1)}, f32[1,1,4,64]{3,2,1,0:T(4,128)S(1)}, u32[]{:S(2)}, u32[]{:S(2)}) collective-permute-start(f32[1,1,4,64]{3,2,1,0:T(4,128)S(1)} %get-tuple-element.59), channel_id=1, source_target_pairs={{0,1},{1,2},{2,3},{3,4},{4,5},{5,6},{6,7},{7,0},{8,9},{9,10},{10,1... | collective-permute-start | bytes 3080 | tf_op jit(solution)/shard_map/ppermute | solution.py:17
  138.6 6.3 %collective-permute-start.21 = (f32[1,1,4,64]{3,2,1,0:T(4,128)S(1)}, f32[1,1,4,64]{3,2,1,0:T(4,128)S(1)}, u32[]{:S(2)}, u32[]{:S(2)}) collective-permute-start(f32[1,1,4,64]{3,2,1,0:T(4,128)S(1)} %get-tuple-element.60), channel_id=1, source_target_pairs={{1,0},{2,1},{3,2},{4,3},{5,4},{6,5},{7,6},{0,7},{9,8},{10,9},{11,1... | collective-permute-start | bytes 3080 | tf_op jit(solution)/shard_map/ppermute | solution.py:19
  195.1 6.5 %collective-permute-start.26 = (f32[1,2,4,64]{3,2,1,0:T(4,128)S(1)}, f32[1,2,4,64]{3,2,1,0:T(4,128)S(1)}, u32[]{:S(2)}, u32[]{:S(2)}) collective-permute-start(f32[1,2,4,64]{3,2,1,0:T(4,128)S(1)} %get-tuple-element.53), channel_id=1, source_target_pairs={{0,8},{8,16},{16,24},{24,0},{1,9},{9,17},{17,25},{25,1},{2,10},{10... | collective-permute-start | bytes 6152 | tf_op jit(solution)/shard_map/ppermute | solution.py:17
  195.1 8.0 %collective-permute-start.27 = (f32[1,2,4,64]{3,2,1,0:T(4,128)S(1)}, f32[1,2,4,64]{3,2,1,0:T(4,128)S(1)}, u32[]{:S(2)}, u32[]{:S(2)}) collective-permute-start(f32[1,2,4,64]{3,2,1,0:T(4,128)S(1)} %get-tuple-element.53), channel_id=1, source_target_pairs={{8,0},{16,8},{24,16},{0,24},{9,1},{17,9},{25,17},{1,25},{10,2},{18... | collective-permute-start | bytes 6152 | tf_op jit(solution)/shard_map/ppermute | solution.py:19
  196.8 6.3 %collective-permute-start.24 = (f32[1,1,4,64]{3,2,1,0:T(4,128)S(1)}, f32[1,1,4,64]{3,2,1,0:T(4,128)S(1)}, u32[]{:S(2)}, u32[]{:S(2)}) collective-permute-start(f32[1,1,4,64]{3,2,1,0:T(4,128)S(1)} %get-tuple-element.55), channel_id=1, source_target_pairs={{0,1},{1,2},{2,3},{3,4},{4,5},{5,6},{6,7},{7,0},{8,9},{9,10},{10,1... | collective-permute-start | bytes 3080 | tf_op jit(solution)/shard_map/ppermute | solution.py:17
  199.1 4.0 collective-permute-start.25
  213.2 6.5 %collective-permute-start.30 = (f32[1,2,4,64]{3,2,1,0:T(4,128)S(1)}, f32[1,2,4,64]{3,2,1,0:T(4,128)S(1)}, u32[]{:S(2)}, u32[]{:S(2)}) collective-permute-start(f32[1,2,4,64]{3,2,1,0:T(4,128)S(1)} %get-tuple-element.49), channel_id=1, source_target_pairs={{0,8},{8,16},{16,24},{24,0},{1,9},{9,17},{17,25},{25,1},{2,10},{10... | collective-permute-start | bytes 6152 | tf_op jit(solution)/shard_map/ppermute | solution.py:17
  213.2 8.0 %collective-permute-start.31 = (f32[1,2,4,64]{3,2,1,0:T(4,128)S(1)}, f32[1,2,4,64]{3,2,1,0:T(4,128)S(1)}, u32[]{:S(2)}, u32[]{:S(2)}) collective-permute-start(f32[1,2,4,64]{3,2,1,0:T(4,128)S(1)} %get-tuple-element.49), channel_id=1, source_target_pairs={{8,0},{16,8},{24,16},{0,24},{9,1},{17,9},{25,17},{1,25},{10,2},{18... | collective-permute-start | bytes 6152 | tf_op jit(solution)/shard_map/ppermute | solution.py:19
  214.9 6.3 %collective-permute-start.28 = (f32[1,1,4,64]{3,2,1,0:T(4,128)S(1)}, f32[1,1,4,64]{3,2,1,0:T(4,128)S(1)}, u32[]{:S(2)}, u32[]{:S(2)}) collective-permute-start(f32[1,1,4,64]{3,2,1,0:T(4,128)S(1)} %get-tuple-element.51), channel_id=1, source_target_pairs={{0,1},{1,2},{2,3},{3,4},{4,5},{5,6},{6,7},{7,0},{8,9},{9,10},{10,1... | collective-permute-start | bytes 3080 | tf_op jit(solution)/shard_map/ppermute | solution.py:17
  216.7 4.5 collective-permute-start.29
  231.0 6.5 %collective-permute-start.34 = (f32[1,2,4,64]{3,2,1,0:T(4,128)S(1)}, f32[1,2,4,64]{3,2,1,0:T(4,128)S(1)}, u32[]{:S(2)}, u32[]{:S(2)}) collective-permute-start(f32[1,2,4,64]{3,2,1,0:T(4,128)S(1)} %get-tuple-element.45), channel_id=1, source_target_pairs={{0,8},{8,16},{16,24},{24,0},{1,9},{9,17},{17,25},{25,1},{2,10},{10... | collective-permute-start | bytes 6152 | tf_op jit(solution)/shard_map/ppermute | solution.py:17
  231.0 8.0 %collective-permute-start.35 = (f32[1,2,4,64]{3,2,1,0:T(4,128)S(1)}, f32[1,2,4,64]{3,2,1,0:T(4,128)S(1)}, u32[]{:S(2)}, u32[]{:S(2)}) collective-permute-start(f32[1,2,4,64]{3,2,1,0:T(4,128)S(1)} %get-tuple-element.45), channel_id=1, source_target_pairs={{8,0},{16,8},{24,16},{0,24},{9,1},{17,9},{25,17},{1,25},{10,2},{18... | collective-permute-start | bytes 6152 | tf_op jit(solution)/shard_map/ppermute | solution.py:19
  232.8 6.3 %collective-permute-start.32 = (f32[1,1,4,64]{3,2,1,0:T(4,128)S(1)}, f32[1,1,4,64]{3,2,1,0:T(4,128)S(1)}, u32[]{:S(2)}, u32[]{:S(2)}) collective-permute-start(f32[1,1,4,64]{3,2,1,0:T(4,128)S(1)} %get-tuple-element.47), channel_id=1, source_target_pairs={{0,1},{1,2},{2,3},{3,4},{4,5},{5,6},{6,7},{7,0},{8,9},{9,10},{10,1... | collective-permute-start | bytes 3080 | tf_op jit(solution)/shard_map/ppermute | solution.py:17
  234.1 4.9 %collective-permute-start.33 = (f32[1,1,4,64]{3,2,1,0:T(4,128)S(1)}, f32[1,1,4,64]{3,2,1,0:T(4,128)S(1)}, u32[]{:S(2)}, u32[]{:S(2)}) collective-permute-start(f32[1,1,4,64]{3,2,1,0:T(4,128)S(1)} %get-tuple-element.48), channel_id=1, source_target_pairs={{1,0},{2,1},{3,2},{4,3},{5,4},{6,5},{7,6},{0,7},{9,8},{10,9},{11,1... | collective-permute-start | bytes 3080 | tf_op jit(solution)/shard_map/ppermute | solution.py:19
  270.4 6.5 %collective-permute-start.38 = (f32[1,2,4,64]{3,2,1,0:T(4,128)S(1)}, f32[1,2,4,64]{3,2,1,0:T(4,128)S(1)}, u32[]{:S(2)}, u32[]{:S(2)}) collective-permute-start(f32[1,2,4,64]{3,2,1,0:T(4,128)S(1)} %get-tuple-element.41), channel_id=1, source_target_pairs={{0,8},{8,16},{16,24},{24,0},{1,9},{9,17},{17,25},{25,1},{2,10},{10... | collective-permute-start | bytes 6152 | tf_op jit(solution)/shard_map/ppermute | solution.py:17
  270.4 8.0 %collective-permute-start.39 = (f32[1,2,4,64]{3,2,1,0:T(4,128)S(1)}, f32[1,2,4,64]{3,2,1,0:T(4,128)S(1)}, u32[]{:S(2)}, u32[]{:S(2)}) collective-permute-start(f32[1,2,4,64]{3,2,1,0:T(4,128)S(1)} %get-tuple-element.41), channel_id=1, source_target_pairs={{8,0},{16,8},{24,16},{0,24},{9,1},{17,9},{25,17},{1,25},{10,2},{18... | collective-permute-start | bytes 6152 | tf_op jit(solution)/shard_map/ppermute | solution.py:19
  272.2 6.3 %collective-permute-start.36 = (f32[1,1,4,64]{3,2,1,0:T(4,128)S(1)}, f32[1,1,4,64]{3,2,1,0:T(4,128)S(1)}, u32[]{:S(2)}, u32[]{:S(2)}) collective-permute-start(f32[1,1,4,64]{3,2,1,0:T(4,128)S(1)} %get-tuple-element.43), channel_id=1, source_target_pairs={{0,1},{1,2},{2,3},{3,4},{4,5},{5,6},{6,7},{7,0},{8,9},{9,10},{10,1... | collective-permute-start | bytes 3080 | tf_op jit(solution)/shard_map/ppermute | solution.py:17
  272.2 6.3 %collective-permute-start.37 = (f32[1,1,4,64]{3,2,1,0:T(4,128)S(1)}, f32[1,1,4,64]{3,2,1,0:T(4,128)S(1)}, u32[]{:S(2)}, u32[]{:S(2)}) collective-permute-start(f32[1,1,4,64]{3,2,1,0:T(4,128)S(1)} %get-tuple-element.44), channel_id=1, source_target_pairs={{1,0},{2,1},{3,2},{4,3},{5,4},{6,5},{7,6},{0,7},{9,8},{10,9},{11,1... | collective-permute-start | bytes 3080 | tf_op jit(solution)/shard_map/ppermute | solution.py:19
  329.3 6.5 %collective-permute-start.42 = (f32[1,2,4,64]{3,2,1,0:T(4,128)S(1)}, f32[1,2,4,64]{3,2,1,0:T(4,128)S(1)}, u32[]{:S(2)}, u32[]{:S(2)}) collective-permute-start(f32[1,2,4,64]{3,2,1,0:T(4,128)S(1)} %get-tuple-element.37), channel_id=1, source_target_pairs={{0,8},{8,16},{16,24},{24,0},{1,9},{9,17},{17,25},{25,1},{2,10},{10... | collective-permute-start | bytes 6152 | tf_op jit(solution)/shard_map/ppermute | solution.py:17
  329.3 8.0 %collective-permute-start.43 = (f32[1,2,4,64]{3,2,1,0:T(4,128)S(1)}, f32[1,2,4,64]{3,2,1,0:T(4,128)S(1)}, u32[]{:S(2)}, u32[]{:S(2)}) collective-permute-start(f32[1,2,4,64]{3,2,1,0:T(4,128)S(1)} %get-tuple-element.37), channel_id=1, source_target_pairs={{8,0},{16,8},{24,16},{0,24},{9,1},{17,9},{25,17},{1,25},{10,2},{18... | collective-permute-start | bytes 6152 | tf_op jit(solution)/shard_map/ppermute | solution.py:19
  331.1 6.3 %collective-permute-start.40 = (f32[1,1,4,64]{3,2,1,0:T(4,128)S(1)}, f32[1,1,4,64]{3,2,1,0:T(4,128)S(1)}, u32[]{:S(2)}, u32[]{:S(2)}) collective-permute-start(f32[1,1,4,64]{3,2,1,0:T(4,128)S(1)} %get-tuple-element.39), channel_id=1, source_target_pairs={{0,1},{1,2},{2,3},{3,4},{4,5},{5,6},{6,7},{7,0},{8,9},{9,10},{10,1... | collective-permute-start | bytes 3080 | tf_op jit(solution)/shard_map/ppermute | solution.py:17
  333.3 4.0 collective-permute-start.41
  347.4 6.5 %collective-permute-start.46 = (f32[1,2,4,64]{3,2,1,0:T(4,128)S(1)}, f32[1,2,4,64]{3,2,1,0:T(4,128)S(1)}, u32[]{:S(2)}, u32[]{:S(2)}) collective-permute-start(f32[1,2,4,64]{3,2,1,0:T(4,128)S(1)} %get-tuple-element.33), channel_id=1, source_target_pairs={{0,8},{8,16},{16,24},{24,0},{1,9},{9,17},{17,25},{25,1},{2,10},{10... | collective-permute-start | bytes 6152 | tf_op jit(solution)/shard_map/ppermute | solution.py:17
  347.4 8.0 %collective-permute-start.47 = (f32[1,2,4,64]{3,2,1,0:T(4,128)S(1)}, f32[1,2,4,64]{3,2,1,0:T(4,128)S(1)}, u32[]{:S(2)}, u32[]{:S(2)}) collective-permute-start(f32[1,2,4,64]{3,2,1,0:T(4,128)S(1)} %get-tuple-element.33), channel_id=1, source_target_pairs={{8,0},{16,8},{24,16},{0,24},{9,1},{17,9},{25,17},{1,25},{10,2},{18... | collective-permute-start | bytes 6152 | tf_op jit(solution)/shard_map/ppermute | solution.py:19
  349.2 6.3 %collective-permute-start.44 = (f32[1,1,4,64]{3,2,1,0:T(4,128)S(1)}, f32[1,1,4,64]{3,2,1,0:T(4,128)S(1)}, u32[]{:S(2)}, u32[]{:S(2)}) collective-permute-start(f32[1,1,4,64]{3,2,1,0:T(4,128)S(1)} %get-tuple-element.35), channel_id=1, source_target_pairs={{0,1},{1,2},{2,3},{3,4},{4,5},{5,6},{6,7},{7,0},{8,9},{9,10},{10,1... | collective-permute-start | bytes 3080 | tf_op jit(solution)/shard_map/ppermute | solution.py:17
  351.0 4.5 collective-permute-start.45
  365.2 6.5 %collective-permute-start.50 = (f32[1,2,4,64]{3,2,1,0:T(4,128)S(1)}, f32[1,2,4,64]{3,2,1,0:T(4,128)S(1)}, u32[]{:S(2)}, u32[]{:S(2)}) collective-permute-start(f32[1,2,4,64]{3,2,1,0:T(4,128)S(1)} %get-tuple-element.29), channel_id=1, source_target_pairs={{0,8},{8,16},{16,24},{24,0},{1,9},{9,17},{17,25},{25,1},{2,10},{10... | collective-permute-start | bytes 6152 | tf_op jit(solution)/shard_map/ppermute | solution.py:17
  365.3 8.0 %collective-permute-start.51 = (f32[1,2,4,64]{3,2,1,0:T(4,128)S(1)}, f32[1,2,4,64]{3,2,1,0:T(4,128)S(1)}, u32[]{:S(2)}, u32[]{:S(2)}) collective-permute-start(f32[1,2,4,64]{3,2,1,0:T(4,128)S(1)} %get-tuple-element.29), channel_id=1, source_target_pairs={{8,0},{16,8},{24,16},{0,24},{9,1},{17,9},{25,17},{1,25},{10,2},{18... | collective-permute-start | bytes 6152 | tf_op jit(solution)/shard_map/ppermute | solution.py:19
  367.0 6.3 %collective-permute-start.48 = (f32[1,1,4,64]{3,2,1,0:T(4,128)S(1)}, f32[1,1,4,64]{3,2,1,0:T(4,128)S(1)}, u32[]{:S(2)}, u32[]{:S(2)}) collective-permute-start(f32[1,1,4,64]{3,2,1,0:T(4,128)S(1)} %get-tuple-element.31), channel_id=1, source_target_pairs={{0,1},{1,2},{2,3},{3,4},{4,5},{5,6},{6,7},{7,0},{8,9},{9,10},{10,1... | collective-permute-start | bytes 3080 | tf_op jit(solution)/shard_map/ppermute | solution.py:17
  368.4 4.9 %collective-permute-start.49 = (f32[1,1,4,64]{3,2,1,0:T(4,128)S(1)}, f32[1,1,4,64]{3,2,1,0:T(4,128)S(1)}, u32[]{:S(2)}, u32[]{:S(2)}) collective-permute-start(f32[1,1,4,64]{3,2,1,0:T(4,128)S(1)} %get-tuple-element.32), channel_id=1, source_target_pairs={{1,0},{2,1},{3,2},{4,3},{5,4},{6,5},{7,6},{0,7},{9,8},{10,9},{11,1... | collective-permute-start | bytes 3080 | tf_op jit(solution)/shard_map/ppermute | solution.py:19
  404.6 6.5 %collective-permute-start.54 = (f32[1,2,4,64]{3,2,1,0:T(4,128)S(1)}, f32[1,2,4,64]{3,2,1,0:T(4,128)S(1)}, u32[]{:S(2)}, u32[]{:S(2)}) collective-permute-start(f32[1,2,4,64]{3,2,1,0:T(4,128)S(1)} %get-tuple-element.25), channel_id=1, source_target_pairs={{0,8},{8,16},{16,24},{24,0},{1,9},{9,17},{17,25},{25,1},{2,10},{10... | collective-permute-start | bytes 6152 | tf_op jit(solution)/shard_map/ppermute | solution.py:17
  404.7 8.0 %collective-permute-start.55 = (f32[1,2,4,64]{3,2,1,0:T(4,128)S(1)}, f32[1,2,4,64]{3,2,1,0:T(4,128)S(1)}, u32[]{:S(2)}, u32[]{:S(2)}) collective-permute-start(f32[1,2,4,64]{3,2,1,0:T(4,128)S(1)} %get-tuple-element.25), channel_id=1, source_target_pairs={{8,0},{16,8},{24,16},{0,24},{9,1},{17,9},{25,17},{1,25},{10,2},{18... | collective-permute-start | bytes 6152 | tf_op jit(solution)/shard_map/ppermute | solution.py:19
  406.4 6.3 %collective-permute-start.52 = (f32[1,1,4,64]{3,2,1,0:T(4,128)S(1)}, f32[1,1,4,64]{3,2,1,0:T(4,128)S(1)}, u32[]{:S(2)}, u32[]{:S(2)}) collective-permute-start(f32[1,1,4,64]{3,2,1,0:T(4,128)S(1)} %get-tuple-element.27), channel_id=1, source_target_pairs={{0,1},{1,2},{2,3},{3,4},{4,5},{5,6},{6,7},{7,0},{8,9},{9,10},{10,1... | collective-permute-start | bytes 3080 | tf_op jit(solution)/shard_map/ppermute | solution.py:17
  406.4 6.3 %collective-permute-start.53 = (f32[1,1,4,64]{3,2,1,0:T(4,128)S(1)}, f32[1,1,4,64]{3,2,1,0:T(4,128)S(1)}, u32[]{:S(2)}, u32[]{:S(2)}) collective-permute-start(f32[1,1,4,64]{3,2,1,0:T(4,128)S(1)} %get-tuple-element.28), channel_id=1, source_target_pairs={{1,0},{2,1},{3,2},{4,3},{5,4},{6,5},{7,6},{0,7},{9,8},{10,9},{11,1... | collective-permute-start | bytes 3080 | tf_op jit(solution)/shard_map/ppermute | solution.py:19
where the time goes:
time: 465 us; the launch traced here: 464 us
  blocking collectives  206 us (44%)
  local copies, waits for them, and re-layouts  139 us (30%)
  starting transfers between devices  92 us (20%)
  waiting for transfers between devices  20.7 us (4%)
    gather x14, local copies, waits for them, and re-layouts, jump(): picked = jnp.take_along_axis(facing, position, axis=-1)  134 us
    psum x3, blocking collectives, global_sums(): return lax.psum((first_dot, second_dot), ('srow', 'scol'))  122 us
    all_gather x4, blocking collectives, apply_inverse(): lax.all_gather(coarse_in, 'scol', axis=0, tiled=True)  84.1 us
    ppermute x28, starting transfers between devices, with_halo(): lax.ppermute(head, axis, [((i + 1) % count, i) for i in range(count)])  78.3 us
    ppermute x28, waiting for transfers between devices, with_halo(): lax.ppermute(tail, axis, [(i, (i + 1) % count) for i in range(count)])  20.7 us
    ppermute x28, starting transfers between devices, with_halo(): lax.ppermute(tail, axis, [(i, (i + 1) % count) for i in range(count)])  13.7 us
  transfers between devices with their start and end apart: 56, of which 14 were waited for; matrix products, arithmetic and copies ran while one was open for 0% of the time, Pallas kernels for 0%

commit v1 on v0

--- a/solution.py
+++ b/solution.py
@@ -5,6 +5,18 @@
 
 ITERS = 3
 precise = lax.Precision.HIGHEST
+
+
+def doubled_up(value, axis, dim):
+    ways, here, hop = (lax.axis_size(axis), lax.axis_index(axis), value.shape[dim])
+    line, have = (value, 1)
+    while have < ways:
+        line = jnp.concatenate(
+            [line, lax.ppermute(line, axis, [(d, (d - have) % ways) for d in range(ways)])],
+            axis=dim,
+        )
+        have = 2 * have
+    return jnp.roll(line, here * hop, axis=dim)
 
 
 def with_halo(cells, sides, width):
@@ -52,7 +64,7 @@
     band_rows = coarse_inverse[0]
     coarse_out = jnp.dot(
         band_rows,
-        lax.all_gather(coarse_in, "scol", axis=0, tiled=True),
+        doubled_up(coarse_in, "scol", 0),
         precision=precise,
         preferred_element_type=jnp.float32,
     )

time: 465 us -> 446 us (0.959)
  blocking collectives: 206 us -> 122 us
  waiting for transfers between devices: 20.7 us -> 54.7 us
  starting transfers between devices: 92 us -> 123 us
    all_gather x4 -> x0, blocking collectives: 84.1 us -> none  [apply_inverse(): lax.all_gather(coarse_in, 'scol', axis=0, tiled=True)]
    ppermute x0 -> x12, waiting for transfers between devices: none -> 34 us  [doubled_up(): lax.ppermute(line, axis, [(d, (d - have) % ways) for d in range(ways)])]
    ppermute x0 -> x12, starting transfers between devices: none -> 22.5 us  [doubled_up(): lax.ppermute(line, axis, [(d, (d - have) % ways) for d in range(ways)])]
    ppermute x28, starting transfers between devices: 13.7 us -> 26.9 us  [with_halo(): lax.ppermute(tail, axis, [(i, (i + 1) % count) for i in range(count)])]
    ppermute x28, starting transfers between devices: 78.3 us -> 73.5 us  [with_halo(): lax.ppermute(head, axis, [((i + 1) % count, i) for i in range(count)])]
  transfers between devices with their start and end apart: 56 -> 68, of which waited for: 14 -> 26; matrix products, arithmetic and copies ran while one was open for 0% -> 0% of each run, Pallas kernels for 0% -> 0%
where the time goes in v1:
time: 446 us
  local copies, waits for them, and re-layouts  138 us (31%)
  starting transfers between devices  123 us (28%)
  blocking collectives  122 us (27%)
  waiting for transfers between devices  54.7 us (12%)
    gather x14, local copies, waits for them, and re-layouts, jump(): picked = jnp.take_along_axis(facing, position, axis=-1)  134 us
    psum x3, blocking collectives, global_sums(): return lax.psum((first_dot, second_dot), ('srow', 'scol'))  122 us
    ppermute x28, starting transfers between devices, with_halo(): lax.ppermute(head, axis, [((i + 1) % count, i) for i in range(count)])  73.5 us
    ppermute x12, waiting for transfers between devices, doubled_up(): lax.ppermute(line, axis, [(d, (d - have) % ways) for d in range(ways)])  34 us
    ppermute x28, starting transfers between devices, with_halo(): lax.ppermute(tail, axis, [(i, (i + 1) % count) for i in range(count)])  26.9 us
    ppermute x12, starting transfers between devices, doubled_up(): lax.ppermute(line, axis, [(d, (d - have) % ways) for d in range(ways)])  22.5 us
    ppermute x28, waiting for transfers between devices, with_halo(): lax.ppermute(tail, axis, [(i, (i + 1) % count) for i in range(count)])  20.6 us
  transfers between devices with their start and end apart: 68, of which 26 were waited for; matrix products, arithmetic and copies ran while one was open for 0% of the time, Pallas kernels for 0%

profile of v1, /device:TPU:0, one launch (start us, length us, event | category | flops | bytes accessed | tf_op | source)
XLA Modules:
  0.0 445.8 jit_solution(7945618859425316530)
XLA Ops:
  2.0 1.9 collective-permute-start.3
  4.0 2.3 collective-permute-start
  6.2 3.1 collective-permute-start.1
  10.9 9.6 %gather_fusion = f32[1024]{0:T(1024)S(1)} fusion(f32[2,4,128]{2,1,0:T(4,128)S(1)} %fusion.69, s32[1024]{0:T(1024)S(1)} %bitcast.180), kind=kCustom, calls=%fused_computation.clone | custom fusion | bytes 20480 | tf_op jit(solution)/shard_map/jit(take_along_axis)/gather | solution.py:55
  21.4 4.8 %collective-permute-start.4 = (f32[2,4]{0,1:T(4,128)S(1)}, f32[2,4]{0,1:T(4,128)S(1)}, u32[]{:S(2)}, u32[]{:S(2)}) collective-permute-start(f32[2,4]{0,1:T(4,128)S(1)} %bitcast.198), channel_id=1, source_target_pairs={{0,7},{1,0},{2,1},{3,2},{4,3},{5,4},{6,5},{7,6},{8,15},{9,8},{10,9... | collective-permute-start | bytes 104 | tf_op jit(solution)/shard_map/ppermute | solution.py:15
  28.4 2.8 collective-permute-done.5
  31.3 4.4 collective-permute-done.6
  36.5 1.7 collective-permute-start.10
  38.2 3.3 collective-permute-start.7
  41.5 3.5 collective-permute-start.8
  46.6 9.6 %gather_fusion.1 = f32[1024]{0:T(1024)S(1)} fusion(f32[2,4,128]{2,1,0:T(4,128)S(1)} %fusion.65, s32[1024]{0:T(1024)S(1)} %bitcast.181), kind=kCustom, calls=%fused_computation.1.clone | custom fusion | bytes 20480 | tf_op jit(solution)/shard_map/jit(take_along_axis)/gather | solution.py:55
  56.3 1.7 collective-permute-start.14
  58.1 4.7 %collective-permute-start.12 = (f32[1,1,4,64]{3,2,1,0:T(4,128)S(1)}, f32[1,1,4,64]{3,2,1,0:T(4,128)S(1)}, u32[]{:S(2)}, u32[]{:S(2)}) collective-permute-start(f32[1,1,4,64]{3,2,1,0:T(4,128)S(1)} %get-tuple-element.73), channel_id=1, source_target_pairs={{1,0},{2,1},{3,2},{4,3},{5,4},{6,5},{7,6},{0,7},{9,8},{10,9},{11,1... | collective-permute-start | bytes 3080 | tf_op jit(solution)/shard_map/ppermute | solution.py:31
  64.5 9.6 %gather_fusion.2 = f32[1024]{0:T(1024)S(1)} fusion(f32[2,4,128]{2,1,0:T(4,128)S(1)} %fusion.61, s32[1024]{0:T(1024)S(1)} %bitcast.182), kind=kCustom, calls=%fused_computation.2.clone | custom fusion | bytes 20480 | tf_op jit(solution)/shard_map/jit(take_along_axis)/gather | solution.py:55
  74.5 1.8 collective-permute-start.18
  76.2 4.7 %collective-permute-start.16 = (f32[1,1,4,64]{3,2,1,0:T(4,128)S(1)}, f32[1,1,4,64]{3,2,1,0:T(4,128)S(1)}, u32[]{:S(2)}, u32[]{:S(2)}) collective-permute-start(f32[1,1,4,64]{3,2,1,0:T(4,128)S(1)} %get-tuple-element.69), channel_id=1, source_target_pairs={{1,0},{2,1},{3,2},{4,3},{5,4},{6,5},{7,6},{0,7},{9,8},{10,9},{11,1... | collective-permute-start | bytes 3080 | tf_op jit(solution)/shard_map/ppermute | solution.py:31
  82.6 9.6 %gather_fusion.3 = f32[1024]{0:T(1024)S(1)} fusion(f32[2,4,128]{2,1,0:T(4,128)S(1)} %fusion.57, s32[1024]{0:T(1024)S(1)} %bitcast.183), kind=kCustom, calls=%fused_computation.3.clone | custom fusion | bytes 20480 | tf_op jit(solution)/shard_map/jit(take_along_axis)/gather | solution.py:55
  92.3 1.7 collective-permute-start.22
  94.1 4.7 %collective-permute-start.20 = (f32[1,1,4,64]{3,2,1,0:T(4,128)S(1)}, f32[1,1,4,64]{3,2,1,0:T(4,128)S(1)}, u32[]{:S(2)}, u32[]{:S(2)}) collective-permute-start(f32[1,1,4,64]{3,2,1,0:T(4,128)S(1)} %get-tuple-element.65), channel_id=1, source_target_pairs={{1,0},{2,1},{3,2},{4,3},{5,4},{6,5},{7,6},{0,7},{9,8},{10,9},{11,1... | collective-permute-start | bytes 3080 | tf_op jit(solution)/shard_map/ppermute | solution.py:31
  100.4 9.6 %gather_fusion.4 = f32[1024]{0:T(1024)S(1)} fusion(f32[2,4,128]{2,1,0:T(4,128)S(1)} %fusion.53, s32[1024]{0:T(1024)S(1)} %bitcast.184), kind=kCustom, calls=%fused_computation.4.clone | custom fusion | bytes 20480 | tf_op jit(solution)/shard_map/jit(take_along_axis)/gather | solution.py:55
  110.3 4.7 %collective-permute-start.23 = (f32[2,4]{0,1:T(4,128)S(1)}, f32[2,4]{0,1:T(4,128)S(1)}, u32[]{:S(2)}, u32[]{:S(2)}) collective-permute-start(f32[2,4]{0,1:T(4,128)S(1)} %bitcast.202), channel_id=1, source_target_pairs={{0,7},{1,0},{2,1},{3,2},{4,3},{5,4},{6,5},{7,6},{8,15},{9,8},{10,9... | collective-permute-start | bytes 104 | tf_op jit(solution)/shard_map/ppermute | solution.py:15
  117.2 2.8 collective-permute-done.24
  120.1 4.5 %collective-permute-done.25 = f32[8,4]{0,1:T(4,128)S(1)} collective-permute-done((f32[8,4]{0,1:T(4,128)S(1)}, f32[8,4]{0,1:T(4,128)S(1)}, u32[]{:S(2)}, u32[]{:S(2)}) %collective-permute-start.25) | collective-permute-done | bytes 160 | tf_op jit(solution)/shard_map/ppermute | solution.py:15
  125.2 1.7 collective-permute-start.29
  127.0 3.3 collective-permute-start.26
  130.2 3.5 collective-permute-start.27
  135.4 9.6 %gather_fusion.5 = f32[1024]{0:T(1024)S(1)} fusion(f32[2,4,128]{2,1,0:T(4,128)S(1)} %fusion.49, s32[1024]{0:T(1024)S(1)} %bitcast.185), kind=kCustom, calls=%fused_computation.5.clone | custom fusion | bytes 20480 | tf_op jit(solution)/shard_map/jit(take_along_axis)/gather | solution.py:55
  145.1 40.2 %all-reduce.2 = (f32[4]{0:T(128)S(1)}, f32[4]{0:T(128)S(1)}) all-reduce(f32[4]{0:T(128)S(1)} %get-tuple-element.9, f32[4]{0:T(128)S(1)} %get-tuple-element.8), channel_id=1, replica_groups=mesh['srow'=4,'scol'=8] {'srow','scol'}, use_global_device_ids=true, to_apply=%region_1.4 | all-reduce | flops 8 | bytes 64 | tf_op jit(solution)/shard_map/psum | solution.py:80
  185.5 1.7 collective-permute-start.33
  187.3 2.3 collective-permute-start.30
  189.6 2.4 collective-permute-start.31
  193.6 9.6 %gather_fusion.6 = f32[1024]{0:T(1024)S(1)} fusion(f32[2,4,128]{2,1,0:T(4,128)S(1)} %fusion.45, s32[1024]{0:T(1024)S(1)} %bitcast.186), kind=kCustom, calls=%fused_computation.6.clone | custom fusion | bytes 20480 | tf_op jit(solution)/shard_map/jit(take_along_axis)/gather | solution.py:55
  203.6 1.8 collective-permute-start.37
  205.4 1.8 collective-permute-start.34
  207.2 2.9 collective-permute-start.35
  211.8 9.6 %gather_fusion.7 = f32[1024]{0:T(1024)S(1)} fusion(f32[2,4,128]{2,1,0:T(4,128)S(1)} %fusion.41, s32[1024]{0:T(1024)S(1)} %bitcast.187), kind=kCustom, calls=%fused_computation.7.clone | custom fusion | bytes 20480 | tf_op jit(solution)/shard_map/jit(take_along_axis)/gather | solution.py:55
  224.6 3.4 collective-permute-start.39
  229.6 9.6 %gather_fusion.8 = f32[1024]{0:T(1024)S(1)} fusion(f32[2,4,128]{2,1,0:T(4,128)S(1)} %fusion.37, s32[1024]{0:T(1024)S(1)} %bitcast.188), kind=kCustom, calls=%fused_computation.8.clone | custom fusion | bytes 20480 | tf_op jit(solution)/shard_map/jit(take_along_axis)/gather | solution.py:55
  239.4 4.7 %collective-permute-start.42 = (f32[2,4]{0,1:T(4,128)S(1)}, f32[2,4]{0,1:T(4,128)S(1)}, u32[]{:S(2)}, u32[]{:S(2)}) collective-permute-start(f32[2,4]{0,1:T(4,128)S(1)} %bitcast.206), channel_id=1, source_target_pairs={{0,7},{1,0},{2,1},{3,2},{4,3},{5,4},{6,5},{7,6},{8,15},{9,8},{10,9... | collective-permute-start | bytes 104 | tf_op jit(solution)/shard_map/ppermute | solution.py:15
  246.5 2.6 collective-permute-done.43
  249.2 4.5 %collective-permute-done.44 = f32[8,4]{0,1:T(4,128)S(1)} collective-permute-done((f32[8,4]{0,1:T(4,128)S(1)}, f32[8,4]{0,1:T(4,128)S(1)}, u32[]{:S(2)}, u32[]{:S(2)}) %collective-permute-start.44) | collective-permute-done | bytes 160 | tf_op jit(solution)/shard_map/ppermute | solution.py:15
  254.4 1.7 collective-permute-start.48
  256.1 3.4 collective-permute-start.45
  259.6 3.5 collective-permute-start.46
  264.7 9.6 %gather_fusion.9 = f32[1024]{0:T(1024)S(1)} fusion(f32[2,4,128]{2,1,0:T(4,128)S(1)} %fusion.33, s32[1024]{0:T(1024)S(1)} %bitcast.189), kind=kCustom, calls=%fused_computation.9.clone | custom fusion | bytes 20480 | tf_op jit(solution)/shard_map/jit(take_along_axis)/gather | solution.py:55
  274.5 40.8 %all-reduce.1 = (f32[4]{0:T(128)S(1)}, f32[4]{0:T(128)S(1)}) all-reduce(f32[4]{0:T(128)S(1)} %get-tuple-element.7, f32[4]{0:T(128)S(1)} %get-tuple-element.6), channel_id=1, replica_groups=mesh['srow'=4,'scol'=8] {'srow','scol'}, use_global_device_ids=true, to_apply=%region_5.8 | all-reduce | flops 8 | bytes 64 | tf_op jit(solution)/shard_map/psum | solution.py:80
  315.5 1.8 collective-permute-start.52
  317.2 2.3 collective-permute-start.49
  319.5 2.4 collective-permute-start.50
  323.6 9.6 %gather_fusion.10 = f32[1024]{0:T(1024)S(1)} fusion(f32[2,4,128]{2,1,0:T(4,128)S(1)} %fusion.29, s32[1024]{0:T(1024)S(1)} %bitcast.190), kind=kCustom, calls=%fused_computation.10.clone | custom fusion | bytes 20480 | tf_op jit(solution)/shard_map/jit(take_along_axis)/gather | solution.py:55
  333.6 1.8 collective-permute-start.56
  335.4 1.8 collective-permute-start.53
  337.1 2.9 collective-permute-start.54
  341.7 9.6 %gather_fusion.11 = f32[1024]{0:T(1024)S(1)} fusion(f32[2,4,128]{2,1,0:T(4,128)S(1)} %fusion.25, s32[1024]{0:T(1024)S(1)} %bitcast.191), kind=kCustom, calls=%fused_computation.11.clone | custom fusion | bytes 20480 | tf_op jit(solution)/shard_map/jit(take_along_axis)/gather | solution.py:55
  354.5 3.4 collective-permute-start.58
  359.5 9.6 %gather_fusion.12 = f32[1024]{0:T(1024)S(1)} fusion(f32[2,4,128]{2,1,0:T(4,128)S(1)} %fusion.21, s32[1024]{0:T(1024)S(1)} %bitcast.192), kind=kCustom, calls=%fused_computation.12.clone | custom fusion | bytes 20480 | tf_op jit(solution)/shard_map/jit(take_along_axis)/gather | solution.py:55
  369.4 4.7 %collective-permute-start.61 = (f32[2,4]{0,1:T(4,128)S(1)}, f32[2,4]{0,1:T(4,128)S(1)}, u32[]{:S(2)}, u32[]{:S(2)}) collective-permute-start(f32[2,4]{0,1:T(4,128)S(1)} %bitcast.210), channel_id=1, source_target_pairs={{0,7},{1,0},{2,1},{3,2},{4,3},{5,4},{6,5},{7,6},{8,15},{9,8},{10,9... | collective-permute-start | bytes 104 | tf_op jit(solution)/shard_map/ppermute | solution.py:15
  376.3 2.8 collective-permute-done.62
  379.2 4.5 %collective-permute-done.63 = f32[8,4]{0,1:T(4,128)S(1)} collective-permute-done((f32[8,4]{0,1:T(4,128)S(1)}, f32[8,4]{0,1:T(4,128)S(1)}, u32[]{:S(2)}, u32[]{:S(2)}) %collective-permute-start.63) | collective-permute-done | bytes 160 | tf_op jit(solution)/shard_map/ppermute | solution.py:15
  384.3 1.7 collective-permute-start.67
  386.1 3.3 collective-permute-start.64
  389.4 3.5 collective-permute-start.65
  394.5 9.6 %gather_fusion.13 = f32[1024]{0:T(1024)S(1)} fusion(f32[2,4,128]{2,1,0:T(4,128)S(1)} %fusion.17, s32[1024]{0:T(1024)S(1)} %bitcast.193), kind=kCustom, calls=%fused_computation.13.clone | custom fusion | bytes 20480 | tf_op jit(solution)/shard_map/jit(take_along_axis)/gather | solution.py:55
  404.3 40.8 %all-reduce = (f32[4]{0:T(128)S(1)}, f32[4]{0:T(128)S(1)}) all-reduce(f32[4]{0:T(128)S(1)} %get-tuple-element.5, f32[4]{0:T(128)S(1)} %get-tuple-element.4), channel_id=1, replica_groups=mesh['srow'=4,'scol'=8] {'srow','scol'}, use_global_device_ids=true, to_apply=%region_9.12 | all-reduce | flops 8 | bytes 64 | tf_op jit(solution)/shard_map/psum | solution.py:80
  (207 shorter events, 47.0 us)
Async XLA Ops:
  1.5 7.9 %collective-permute-start.2 = (f32[1,2,4,64]{3,2,1,0:T(4,128)S(1)}, f32[1,2,4,64]{3,2,1,0:T(4,128)S(1)}, u32[]{:S(2)}, u32[]{:S(2)}) collective-permute-start(f32[1,2,4,64]{3,2,1,0:T(4,128)S(1)} %get-tuple-element.78), channel_id=1, source_target_pairs={{0,8},{8,16},{16,24},{24,0},{1,9},{9,17},{17,25},{25,1},{2,10},{10... | collective-permute-start | bytes 6152 | tf_op jit(solution)/shard_map/ppermute | solution.py:29
  2.0 8.8 %collective-permute-start.3 = (f32[1,2,4,64]{3,2,1,0:T(4,128)S(1)}, f32[1,2,4,64]{3,2,1,0:T(4,128)S(1)}, u32[]{:S(2)}, u32[]{:S(2)}) collective-permute-start(f32[1,2,4,64]{3,2,1,0:T(4,128)S(1)} %get-tuple-element.78), channel_id=1, source_target_pairs={{8,0},{16,8},{24,16},{0,24},{9,1},{17,9},{25,17},{1,25},{10,2},{18... | collective-permute-start | bytes 6152 | tf_op jit(solution)/shard_map/ppermute | solution.py:31
  4.0 6.9 %collective-permute-start = (f32[1,1,4,64]{3,2,1,0:T(4,128)S(1)}, f32[1,1,4,64]{3,2,1,0:T(4,128)S(1)}, u32[]{:S(2)}, u32[]{:S(2)}) collective-permute-start(f32[1,1,4,64]{3,2,1,0:T(4,128)S(1)} %get-tuple-element.80), channel_id=1, source_target_pairs={{0,1},{1,2},{2,3},{3,4},{4,5},{5,6},{6,7},{7,0},{8,9},{9,10},{10,1... | collective-permute-start | bytes 3080 | tf_op jit(solution)/shard_map/ppermute | solution.py:29
  6.2 4.6 %collective-permute-start.1 = (f32[1,1,4,64]{3,2,1,0:T(4,128)S(1)}, f32[1,1,4,64]{3,2,1,0:T(4,128)S(1)}, u32[]{:S(2)}, u32[]{:S(2)}) collective-permute-start(f32[1,1,4,64]{3,2,1,0:T(4,128)S(1)} %get-tuple-element.81), channel_id=1, source_target_pairs={{1,0},{2,1},{3,2},{4,3},{5,4},{6,5},{7,6},{0,7},{9,8},{10,9},{11,1... | collective-permute-start | bytes 3080 | tf_op jit(solution)/shard_map/ppermute | solution.py:31
  21.4 6.1 %collective-permute-start.4 = (f32[2,4]{0,1:T(4,128)S(1)}, f32[2,4]{0,1:T(4,128)S(1)}, u32[]{:S(2)}, u32[]{:S(2)}) collective-permute-start(f32[2,4]{0,1:T(4,128)S(1)} %bitcast.198), channel_id=1, source_target_pairs={{0,7},{1,0},{2,1},{3,2},{4,3},{5,4},{6,5},{7,6},{8,15},{9,8},{10,9... | collective-permute-start | bytes 104 | tf_op jit(solution)/shard_map/ppermute | solution.py:15
  31.3 4.5 %collective-permute-start.6 = (f32[8,4]{0,1:T(4,128)S(1)}, f32[8,4]{0,1:T(4,128)S(1)}, u32[]{:S(2)}, u32[]{:S(2)}) collective-permute-start(f32[8,4]{0,1:T(4,128)S(1)} %pad_maximum_fusion.15), channel_id=1, source_target_pairs={{0,4},{1,5},{2,6},{3,7},{4,0},{5,1},{6,2},{7,3},{8,12},{9,13},{10,... | collective-permute-start | bytes 392 | tf_op jit(solution)/shard_map/ppermute | solution.py:15
  36.4 8.5 %collective-permute-start.9 = (f32[1,2,4,64]{3,2,1,0:T(4,128)S(1)}, f32[1,2,4,64]{3,2,1,0:T(4,128)S(1)}, u32[]{:S(2)}, u32[]{:S(2)}) collective-permute-start(f32[1,2,4,64]{3,2,1,0:T(4,128)S(1)} %get-tuple-element.74), channel_id=1, source_target_pairs={{0,8},{8,16},{16,24},{24,0},{1,9},{9,17},{17,25},{25,1},{2,10},{10... | collective-permute-start | bytes 6152 | tf_op jit(solution)/shard_map/ppermute | solution.py:29
  36.5 10.1 %collective-permute-start.10 = (f32[1,2,4,64]{3,2,1,0:T(4,128)S(1)}, f32[1,2,4,64]{3,2,1,0:T(4,128)S(1)}, u32[]{:S(2)}, u32[]{:S(2)}) collective-permute-start(f32[1,2,4,64]{3,2,1,0:T(4,128)S(1)} %get-tuple-element.74), channel_id=1, source_target_pairs={{8,0},{16,8},{24,16},{0,24},{9,1},{17,9},{25,17},{1,25},{10,2},{18... | collective-permute-start | bytes 6152 | tf_op jit(solution)/shard_map/ppermute | solution.py:31
  38.2 8.3 %collective-permute-start.7 = (f32[1,1,4,64]{3,2,1,0:T(4,128)S(1)}, f32[1,1,4,64]{3,2,1,0:T(4,128)S(1)}, u32[]{:S(2)}, u32[]{:S(2)}) collective-permute-start(f32[1,1,4,64]{3,2,1,0:T(4,128)S(1)} %get-tuple-element.76), channel_id=1, source_target_pairs={{0,1},{1,2},{2,3},{3,4},{4,5},{5,6},{6,7},{7,0},{8,9},{9,10},{10,1... | collective-permute-start | bytes 3080 | tf_op jit(solution)/shard_map/ppermute | solution.py:29
  41.5 5.1 %collective-permute-start.8 = (f32[1,1,4,64]{3,2,1,0:T(4,128)S(1)}, f32[1,1,4,64]{3,2,1,0:T(4,128)S(1)}, u32[]{:S(2)}, u32[]{:S(2)}) collective-permute-start(f32[1,1,4,64]{3,2,1,0:T(4,128)S(1)} %get-tuple-element.77), channel_id=1, source_target_pairs={{1,0},{2,1},{3,2},{4,3},{5,4},{6,5},{7,6},{0,7},{9,8},{10,9},{11,1... | collective-permute-start | bytes 3080 | tf_op jit(solution)/shard_map/ppermute | solution.py:31
  56.3 6.5 %collective-permute-start.13 = (f32[1,2,4,64]{3,2,1,0:T(4,128)S(1)}, f32[1,2,4,64]{3,2,1,0:T(4,128)S(1)}, u32[]{:S(2)}, u32[]{:S(2)}) collective-permute-start(f32[1,2,4,64]{3,2,1,0:T(4,128)S(1)} %get-tuple-element.70), channel_id=1, source_target_pairs={{0,8},{8,16},{16,24},{24,0},{1,9},{9,17},{17,25},{25,1},{2,10},{10... | collective-permute-start | bytes 6152 | tf_op jit(solution)/shard_map/ppermute | solution.py:29
  56.3 8.0 %collective-permute-start.14 = (f32[1,2,4,64]{3,2,1,0:T(4,128)S(1)}, f32[1,2,4,64]{3,2,1,0:T(4,128)S(1)}, u32[]{:S(2)}, u32[]{:S(2)}) collective-permute-start(f32[1,2,4,64]{3,2,1,0:T(4,128)S(1)} %get-tuple-element.70), channel_id=1, source_target_pairs={{8,0},{16,8},{24,16},{0,24},{9,1},{17,9},{25,17},{1,25},{10,2},{18... | collective-permute-start | bytes 6152 | tf_op jit(solution)/shard_map/ppermute | solution.py:31
  58.1 6.3 %collective-permute-start.11 = (f32[1,1,4,64]{3,2,1,0:T(4,128)S(1)}, f32[1,1,4,64]{3,2,1,0:T(4,128)S(1)}, u32[]{:S(2)}, u32[]{:S(2)}) collective-permute-start(f32[1,1,4,64]{3,2,1,0:T(4,128)S(1)} %get-tuple-element.72), channel_id=1, source_target_pairs={{0,1},{1,2},{2,3},{3,4},{4,5},{5,6},{6,7},{7,0},{8,9},{9,10},{10,1... | collective-permute-start | bytes 3080 | tf_op jit(solution)/shard_map/ppermute | solution.py:29
  58.1 6.3 %collective-permute-start.12 = (f32[1,1,4,64]{3,2,1,0:T(4,128)S(1)}, f32[1,1,4,64]{3,2,1,0:T(4,128)S(1)}, u32[]{:S(2)}, u32[]{:S(2)}) collective-permute-start(f32[1,1,4,64]{3,2,1,0:T(4,128)S(1)} %get-tuple-element.73), channel_id=1, source_target_pairs={{1,0},{2,1},{3,2},{4,3},{5,4},{6,5},{7,6},{0,7},{9,8},{10,9},{11,1... | collective-permute-start | bytes 3080 | tf_op jit(solution)/shard_map/ppermute | solution.py:31
  74.5 6.5 %collective-permute-start.17 = (f32[1,2,4,64]{3,2,1,0:T(4,128)S(1)}, f32[1,2,4,64]{3,2,1,0:T(4,128)S(1)}, u32[]{:S(2)}, u32[]{:S(2)}) collective-permute-start(f32[1,2,4,64]{3,2,1,0:T(4,128)S(1)} %get-tuple-element.66), channel_id=1, source_target_pairs={{0,8},{8,16},{16,24},{24,0},{1,9},{9,17},{17,25},{25,1},{2,10},{10... | collective-permute-start | bytes 6152 | tf_op jit(solution)/shard_map/ppermute | solution.py:29
  74.5 8.0 %collective-permute-start.18 = (f32[1,2,4,64]{3,2,1,0:T(4,128)S(1)}, f32[1,2,4,64]{3,2,1,0:T(4,128)S(1)}, u32[]{:S(2)}, u32[]{:S(2)}) collective-permute-start(f32[1,2,4,64]{3,2,1,0:T(4,128)S(1)} %get-tuple-element.66), channel_id=1, source_target_pairs={{8,0},{16,8},{24,16},{0,24},{9,1},{17,9},{25,17},{1,25},{10,2},{18... | collective-permute-start | bytes 6152 | tf_op jit(solution)/shard_map/ppermute | solution.py:31
  76.2 6.3 %collective-permute-start.15 = (f32[1,1,4,64]{3,2,1,0:T(4,128)S(1)}, f32[1,1,4,64]{3,2,1,0:T(4,128)S(1)}, u32[]{:S(2)}, u32[]{:S(2)}) collective-permute-start(f32[1,1,4,64]{3,2,1,0:T(4,128)S(1)} %get-tuple-element.68), channel_id=1, source_target_pairs={{0,1},{1,2},{2,3},{3,4},{4,5},{5,6},{6,7},{7,0},{8,9},{9,10},{10,1... | collective-permute-start | bytes 3080 | tf_op jit(solution)/shard_map/ppermute | solution.py:29
  76.2 6.3 %collective-permute-start.16 = (f32[1,1,4,64]{3,2,1,0:T(4,128)S(1)}, f32[1,1,4,64]{3,2,1,0:T(4,128)S(1)}, u32[]{:S(2)}, u32[]{:S(2)}) collective-permute-start(f32[1,1,4,64]{3,2,1,0:T(4,128)S(1)} %get-tuple-element.69), channel_id=1, source_target_pairs={{1,0},{2,1},{3,2},{4,3},{5,4},{6,5},{7,6},{0,7},{9,8},{10,9},{11,1... | collective-permute-start | bytes 3080 | tf_op jit(solution)/shard_map/ppermute | solution.py:31
  92.3 6.5 %collective-permute-start.21 = (f32[1,2,4,64]{3,2,1,0:T(4,128)S(1)}, f32[1,2,4,64]{3,2,1,0:T(4,128)S(1)}, u32[]{:S(2)}, u32[]{:S(2)}) collective-permute-start(f32[1,2,4,64]{3,2,1,0:T(4,128)S(1)} %get-tuple-element.62), channel_id=1, source_target_pairs={{0,8},{8,16},{16,24},{24,0},{1,9},{9,17},{17,25},{25,1},{2,10},{10... | collective-permute-start | bytes 6152 | tf_op jit(solution)/shard_map/ppermute | solution.py:29
  92.3 8.0 %collective-permute-start.22 = (f32[1,2,4,64]{3,2,1,0:T(4,128)S(1)}, f32[1,2,4,64]{3,2,1,0:T(4,128)S(1)}, u32[]{:S(2)}, u32[]{:S(2)}) collective-permute-start(f32[1,2,4,64]{3,2,1,0:T(4,128)S(1)} %get-tuple-element.62), channel_id=1, source_target_pairs={{8,0},{16,8},{24,16},{0,24},{9,1},{17,9},{25,17},{1,25},{10,2},{18... | collective-permute-start | bytes 6152 | tf_op jit(solution)/shard_map/ppermute | solution.py:31
  94.0 6.3 %collective-permute-start.19 = (f32[1,1,4,64]{3,2,1,0:T(4,128)S(1)}, f32[1,1,4,64]{3,2,1,0:T(4,128)S(1)}, u32[]{:S(2)}, u32[]{:S(2)}) collective-permute-start(f32[1,1,4,64]{3,2,1,0:T(4,128)S(1)} %get-tuple-element.64), channel_id=1, source_target_pairs={{0,1},{1,2},{2,3},{3,4},{4,5},{5,6},{6,7},{7,0},{8,9},{9,10},{10,1... | collective-permute-start | bytes 3080 | tf_op jit(solution)/shard_map/ppermute | solution.py:29
  94.1 6.3 %collective-permute-start.20 = (f32[1,1,4,64]{3,2,1,0:T(4,128)S(1)}, f32[1,1,4,64]{3,2,1,0:T(4,128)S(1)}, u32[]{:S(2)}, u32[]{:S(2)}) collective-permute-start(f32[1,1,4,64]{3,2,1,0:T(4,128)S(1)} %get-tuple-element.65), channel_id=1, source_target_pairs={{1,0},{2,1},{3,2},{4,3},{5,4},{6,5},{7,6},{0,7},{9,8},{10,9},{11,1... | collective-permute-start | bytes 3080 | tf_op jit(solution)/shard_map/ppermute | solution.py:31
  110.3 6.0 %collective-permute-start.23 = (f32[2,4]{0,1:T(4,128)S(1)}, f32[2,4]{0,1:T(4,128)S(1)}, u32[]{:S(2)}, u32[]{:S(2)}) collective-permute-start(f32[2,4]{0,1:T(4,128)S(1)} %bitcast.202), channel_id=1, source_target_pairs={{0,7},{1,0},{2,1},{3,2},{4,3},{5,4},{6,5},{7,6},{8,15},{9,8},{10,9... | collective-permute-start | bytes 104 | tf_op jit(solution)/shard_map/ppermute | solution.py:15
  120.0 4.5 %collective-permute-start.25 = (f32[8,4]{0,1:T(4,128)S(1)}, f32[8,4]{0,1:T(4,128)S(1)}, u32[]{:S(2)}, u32[]{:S(2)}) collective-permute-start(f32[8,4]{0,1:T(4,128)S(1)} %pad_maximum_fusion.17), channel_id=1, source_target_pairs={{0,4},{1,5},{2,6},{3,7},{4,0},{5,1},{6,2},{7,3},{8,12},{9,13},{10,... | collective-permute-start | bytes 392 | tf_op jit(solution)/shard_map/ppermute | solution.py:15
  125.2 8.5 %collective-permute-start.28 = (f32[1,2,4,64]{3,2,1,0:T(4,128)S(1)}, f32[1,2,4,64]{3,2,1,0:T(4,128)S(1)}, u32[]{:S(2)}, u32[]{:S(2)}) collective-permute-start(f32[1,2,4,64]{3,2,1,0:T(4,128)S(1)} %get-tuple-element.58), channel_id=1, source_target_pairs={{0,8},{8,16},{16,24},{24,0},{1,9},{9,17},{17,25},{25,1},{2,10},{10... | collective-permute-start | bytes 6152 | tf_op jit(solution)/shard_map/ppermute | solution.py:29
  125.2 10.1 %collective-permute-start.29 = (f32[1,2,4,64]{3,2,1,0:T(4,128)S(1)}, f32[1,2,4,64]{3,2,1,0:T(4,128)S(1)}, u32[]{:S(2)}, u32[]{:S(2)}) collective-permute-start(f32[1,2,4,64]{3,2,1,0:T(4,128)S(1)} %get-tuple-element.58), channel_id=1, source_target_pairs={{8,0},{16,8},{24,16},{0,24},{9,1},{17,9},{25,17},{1,25},{10,2},{18... | collective-permute-start | bytes 6152 | tf_op jit(solution)/shard_map/ppermute | solution.py:31
  127.0 8.3 %collective-permute-start.26 = (f32[1,1,4,64]{3,2,1,0:T(4,128)S(1)}, f32[1,1,4,64]{3,2,1,0:T(4,128)S(1)}, u32[]{:S(2)}, u32[]{:S(2)}) collective-permute-start(f32[1,1,4,64]{3,2,1,0:T(4,128)S(1)} %get-tuple-element.60), channel_id=1, source_target_pairs={{0,1},{1,2},{2,3},{3,4},{4,5},{5,6},{6,7},{7,0},{8,9},{9,10},{10,1... | collective-permute-start | bytes 3080 | tf_op jit(solution)/shard_map/ppermute | solution.py:29
  130.2 5.1 %collective-permute-start.27 = (f32[1,1,4,64]{3,2,1,0:T(4,128)S(1)}, f32[1,1,4,64]{3,2,1,0:T(4,128)S(1)}, u32[]{:S(2)}, u32[]{:S(2)}) collective-permute-start(f32[1,1,4,64]{3,2,1,0:T(4,128)S(1)} %get-tuple-element.61), channel_id=1, source_target_pairs={{1,0},{2,1},{3,2},{4,3},{5,4},{6,5},{7,6},{0,7},{9,8},{10,9},{11,1... | collective-permute-start | bytes 3080 | tf_op jit(solution)/shard_map/ppermute | solution.py:31
  185.5 6.5 %collective-permute-start.32 = (f32[1,2,4,64]{3,2,1,0:T(4,128)S(1)}, f32[1,2,4,64]{3,2,1,0:T(4,128)S(1)}, u32[]{:S(2)}, u32[]{:S(2)}) collective-permute-start(f32[1,2,4,64]{3,2,1,0:T(4,128)S(1)} %get-tuple-element.54), channel_id=1, source_target_pairs={{0,8},{8,16},{16,24},{24,0},{1,9},{9,17},{17,25},{25,1},{2,10},{10... | collective-permute-start | bytes 6152 | tf_op jit(solution)/shard_map/ppermute | solution.py:29
  185.5 8.0 %collective-permute-start.33 = (f32[1,2,4,64]{3,2,1,0:T(4,128)S(1)}, f32[1,2,4,64]{3,2,1,0:T(4,128)S(1)}, u32[]{:S(2)}, u32[]{:S(2)}) collective-permute-start(f32[1,2,4,64]{3,2,1,0:T(4,128)S(1)} %get-tuple-element.54), channel_id=1, source_target_pairs={{8,0},{16,8},{24,16},{0,24},{9,1},{17,9},{25,17},{1,25},{10,2},{18... | collective-permute-start | bytes 6152 | tf_op jit(solution)/shard_map/ppermute | solution.py:31
  187.3 6.3 %collective-permute-start.30 = (f32[1,1,4,64]{3,2,1,0:T(4,128)S(1)}, f32[1,1,4,64]{3,2,1,0:T(4,128)S(1)}, u32[]{:S(2)}, u32[]{:S(2)}) collective-permute-start(f32[1,1,4,64]{3,2,1,0:T(4,128)S(1)} %get-tuple-element.56), channel_id=1, source_target_pairs={{0,1},{1,2},{2,3},{3,4},{4,5},{5,6},{6,7},{7,0},{8,9},{9,10},{10,1... | collective-permute-start | bytes 3080 | tf_op jit(solution)/shard_map/ppermute | solution.py:29
  189.6 4.0 collective-permute-start.31
  203.6 6.5 %collective-permute-start.36 = (f32[1,2,4,64]{3,2,1,0:T(4,128)S(1)}, f32[1,2,4,64]{3,2,1,0:T(4,128)S(1)}, u32[]{:S(2)}, u32[]{:S(2)}) collective-permute-start(f32[1,2,4,64]{3,2,1,0:T(4,128)S(1)} %get-tuple-element.50), channel_id=1, source_target_pairs={{0,8},{8,16},{16,24},{24,0},{1,9},{9,17},{17,25},{25,1},{2,10},{10... | collective-permute-start | bytes 6152 | tf_op jit(solution)/shard_map/ppermute | solution.py:29
  203.6 8.0 %collective-permute-start.37 = (f32[1,2,4,64]{3,2,1,0:T(4,128)S(1)}, f32[1,2,4,64]{3,2,1,0:T(4,128)S(1)}, u32[]{:S(2)}, u32[]{:S(2)}) collective-permute-start(f32[1,2,4,64]{3,2,1,0:T(4,128)S(1)} %get-tuple-element.50), channel_id=1, source_target_pairs={{8,0},{16,8},{24,16},{0,24},{9,1},{17,9},{25,17},{1,25},{10,2},{18... | collective-permute-start | bytes 6152 | tf_op jit(solution)/shard_map/ppermute | solution.py:31
  205.4 6.3 %collective-permute-start.34 = (f32[1,1,4,64]{3,2,1,0:T(4,128)S(1)}, f32[1,1,4,64]{3,2,1,0:T(4,128)S(1)}, u32[]{:S(2)}, u32[]{:S(2)}) collective-permute-start(f32[1,1,4,64]{3,2,1,0:T(4,128)S(1)} %get-tuple-element.52), channel_id=1, source_target_pairs={{0,1},{1,2},{2,3},{3,4},{4,5},{5,6},{6,7},{7,0},{8,9},{9,10},{10,1... | collective-permute-start | bytes 3080 | tf_op jit(solution)/shard_map/ppermute | solution.py:29
  207.2 4.5 %collective-permute-start.35 = (f32[1,1,4,64]{3,2,1,0:T(4,128)S(1)}, f32[1,1,4,64]{3,2,1,0:T(4,128)S(1)}, u32[]{:S(2)}, u32[]{:S(2)}) collective-permute-start(f32[1,1,4,64]{3,2,1,0:T(4,128)S(1)} %get-tuple-element.53), channel_id=1, source_target_pairs={{1,0},{2,1},{3,2},{4,3},{5,4},{6,5},{7,6},{0,7},{9,8},{10,9},{11,1... | collective-permute-start | bytes 3080 | tf_op jit(solution)/shard_map/ppermute | solution.py:31
  221.5 6.5 %collective-permute-start.40 = (f32[1,2,4,64]{3,2,1,0:T(4,128)S(1)}, f32[1,2,4,64]{3,2,1,0:T(4,128)S(1)}, u32[]{:S(2)}, u32[]{:S(2)}) collective-permute-start(f32[1,2,4,64]{3,2,1,0:T(4,128)S(1)} %get-tuple-element.46), channel_id=1, source_target_pairs={{0,8},{8,16},{16,24},{24,0},{1,9},{9,17},{17,25},{25,1},{2,10},{10... | collective-permute-start | bytes 6152 | tf_op jit(solution)/shard_map/ppermute | solution.py:29
  221.5 8.0 %collective-permute-start.41 = (f32[1,2,4,64]{3,2,1,0:T(4,128)S(1)}, f32[1,2,4,64]{3,2,1,0:T(4,128)S(1)}, u32[]{:S(2)}, u32[]{:S(2)}) collective-permute-start(f32[1,2,4,64]{3,2,1,0:T(4,128)S(1)} %get-tuple-element.46), channel_id=1, source_target_pairs={{8,0},{16,8},{24,16},{0,24},{9,1},{17,9},{25,17},{1,25},{10,2},{18... | collective-permute-start | bytes 6152 | tf_op jit(solution)/shard_map/ppermute | solution.py:31
  223.2 6.3 %collective-permute-start.38 = (f32[1,1,4,64]{3,2,1,0:T(4,128)S(1)}, f32[1,1,4,64]{3,2,1,0:T(4,128)S(1)}, u32[]{:S(2)}, u32[]{:S(2)}) collective-permute-start(f32[1,1,4,64]{3,2,1,0:T(4,128)S(1)} %get-tuple-element.48), channel_id=1, source_target_pairs={{0,1},{1,2},{2,3},{3,4},{4,5},{5,6},{6,7},{7,0},{8,9},{9,10},{10,1... | collective-permute-start | bytes 3080 | tf_op jit(solution)/shard_map/ppermute | solution.py:29
  224.6 4.9 %collective-permute-start.39 = (f32[1,1,4,64]{3,2,1,0:T(4,128)S(1)}, f32[1,1,4,64]{3,2,1,0:T(4,128)S(1)}, u32[]{:S(2)}, u32[]{:S(2)}) collective-permute-start(f32[1,1,4,64]{3,2,1,0:T(4,128)S(1)} %get-tuple-element.49), channel_id=1, source_target_pairs={{1,0},{2,1},{3,2},{4,3},{5,4},{6,5},{7,6},{0,7},{9,8},{10,9},{11,1... | collective-permute-start | bytes 3080 | tf_op jit(solution)/shard_map/ppermute | solution.py:31
  239.4 6.0 %collective-permute-start.42 = (f32[2,4]{0,1:T(4,128)S(1)}, f32[2,4]{0,1:T(4,128)S(1)}, u32[]{:S(2)}, u32[]{:S(2)}) collective-permute-start(f32[2,4]{0,1:T(4,128)S(1)} %bitcast.206), channel_id=1, source_target_pairs={{0,7},{1,0},{2,1},{3,2},{4,3},{5,4},{6,5},{7,6},{8,15},{9,8},{10,9... | collective-permute-start | bytes 104 | tf_op jit(solution)/shard_map/ppermute | solution.py:15
  249.2 4.5 %collective-permute-start.44 = (f32[8,4]{0,1:T(4,128)S(1)}, f32[8,4]{0,1:T(4,128)S(1)}, u32[]{:S(2)}, u32[]{:S(2)}) collective-permute-start(f32[8,4]{0,1:T(4,128)S(1)} %pad_maximum_fusion.19), channel_id=1, source_target_pairs={{0,4},{1,5},{2,6},{3,7},{4,0},{5,1},{6,2},{7,3},{8,12},{9,13},{10,... | collective-permute-start | bytes 392 | tf_op jit(solution)/shard_map/ppermute | solution.py:15
  254.4 8.7 %collective-permute-start.47 = (f32[1,2,4,64]{3,2,1,0:T(4,128)S(1)}, f32[1,2,4,64]{3,2,1,0:T(4,128)S(1)}, u32[]{:S(2)}, u32[]{:S(2)}) collective-permute-start(f32[1,2,4,64]{3,2,1,0:T(4,128)S(1)} %get-tuple-element.42), channel_id=1, source_target_pairs={{0,8},{8,16},{16,24},{24,0},{1,9},{9,17},{17,25},{25,1},{2,10},{10... | collective-permute-start | bytes 6152 | tf_op jit(solution)/shard_map/ppermute | solution.py:29
  254.4 10.2 %collective-permute-start.48 = (f32[1,2,4,64]{3,2,1,0:T(4,128)S(1)}, f32[1,2,4,64]{3,2,1,0:T(4,128)S(1)}, u32[]{:S(2)}, u32[]{:S(2)}) collective-permute-start(f32[1,2,4,64]{3,2,1,0:T(4,128)S(1)} %get-tuple-element.42), channel_id=1, source_target_pairs={{8,0},{16,8},{24,16},{0,24},{9,1},{17,9},{25,17},{1,25},{10,2},{18... | collective-permute-start | bytes 6152 | tf_op jit(solution)/shard_map/ppermute | solution.py:31
  256.1 8.5 %collective-permute-start.45 = (f32[1,1,4,64]{3,2,1,0:T(4,128)S(1)}, f32[1,1,4,64]{3,2,1,0:T(4,128)S(1)}, u32[]{:S(2)}, u32[]{:S(2)}) collective-permute-start(f32[1,1,4,64]{3,2,1,0:T(4,128)S(1)} %get-tuple-element.44), channel_id=1, source_target_pairs={{0,1},{1,2},{2,3},{3,4},{4,5},{5,6},{6,7},{7,0},{8,9},{9,10},{10,1... | collective-permute-start | bytes 3080 | tf_op jit(solution)/shard_map/ppermute | solution.py:29
  259.6 5.1 %collective-permute-start.46 = (f32[1,1,4,64]{3,2,1,0:T(4,128)S(1)}, f32[1,1,4,64]{3,2,1,0:T(4,128)S(1)}, u32[]{:S(2)}, u32[]{:S(2)}) collective-permute-start(f32[1,1,4,64]{3,2,1,0:T(4,128)S(1)} %get-tuple-element.45), channel_id=1, source_target_pairs={{1,0},{2,1},{3,2},{4,3},{5,4},{6,5},{7,6},{0,7},{9,8},{10,9},{11,1... | collective-permute-start | bytes 3080 | tf_op jit(solution)/shard_map/ppermute | solution.py:31
  315.5 6.5 %collective-permute-start.51 = (f32[1,2,4,64]{3,2,1,0:T(4,128)S(1)}, f32[1,2,4,64]{3,2,1,0:T(4,128)S(1)}, u32[]{:S(2)}, u32[]{:S(2)}) collective-permute-start(f32[1,2,4,64]{3,2,1,0:T(4,128)S(1)} %get-tuple-element.38), channel_id=1, source_target_pairs={{0,8},{8,16},{16,24},{24,0},{1,9},{9,17},{17,25},{25,1},{2,10},{10... | collective-permute-start | bytes 6152 | tf_op jit(solution)/shard_map/ppermute | solution.py:29
  315.5 8.0 %collective-permute-start.52 = (f32[1,2,4,64]{3,2,1,0:T(4,128)S(1)}, f32[1,2,4,64]{3,2,1,0:T(4,128)S(1)}, u32[]{:S(2)}, u32[]{:S(2)}) collective-permute-start(f32[1,2,4,64]{3,2,1,0:T(4,128)S(1)} %get-tuple-element.38), channel_id=1, source_target_pairs={{8,0},{16,8},{24,16},{0,24},{9,1},{17,9},{25,17},{1,25},{10,2},{18... | collective-permute-start | bytes 6152 | tf_op jit(solution)/shard_map/ppermute | solution.py:31
  317.2 6.3 %collective-permute-start.49 = (f32[1,1,4,64]{3,2,1,0:T(4,128)S(1)}, f32[1,1,4,64]{3,2,1,0:T(4,128)S(1)}, u32[]{:S(2)}, u32[]{:S(2)}) collective-permute-start(f32[1,1,4,64]{3,2,1,0:T(4,128)S(1)} %get-tuple-element.40), channel_id=1, source_target_pairs={{0,1},{1,2},{2,3},{3,4},{4,5},{5,6},{6,7},{7,0},{8,9},{9,10},{10,1... | collective-permute-start | bytes 3080 | tf_op jit(solution)/shard_map/ppermute | solution.py:29
  319.5 4.0 collective-permute-start.50
  333.6 6.5 %collective-permute-start.55 = (f32[1,2,4,64]{3,2,1,0:T(4,128)S(1)}, f32[1,2,4,64]{3,2,1,0:T(4,128)S(1)}, u32[]{:S(2)}, u32[]{:S(2)}) collective-permute-start(f32[1,2,4,64]{3,2,1,0:T(4,128)S(1)} %get-tuple-element.34), channel_id=1, source_target_pairs={{0,8},{8,16},{16,24},{24,0},{1,9},{9,17},{17,25},{25,1},{2,10},{10... | collective-permute-start | bytes 6152 | tf_op jit(solution)/shard_map/ppermute | solution.py:29
  333.6 8.0 %collective-permute-start.56 = (f32[1,2,4,64]{3,2,1,0:T(4,128)S(1)}, f32[1,2,4,64]{3,2,1,0:T(4,128)S(1)}, u32[]{:S(2)}, u32[]{:S(2)}) collective-permute-start(f32[1,2,4,64]{3,2,1,0:T(4,128)S(1)} %get-tuple-element.34), channel_id=1, source_target_pairs={{8,0},{16,8},{24,16},{0,24},{9,1},{17,9},{25,17},{1,25},{10,2},{18... | collective-permute-start | bytes 6152 | tf_op jit(solution)/shard_map/ppermute | solution.py:31
  335.4 6.3 %collective-permute-start.53 = (f32[1,1,4,64]{3,2,1,0:T(4,128)S(1)}, f32[1,1,4,64]{3,2,1,0:T(4,128)S(1)}, u32[]{:S(2)}, u32[]{:S(2)}) collective-permute-start(f32[1,1,4,64]{3,2,1,0:T(4,128)S(1)} %get-tuple-element.36), channel_id=1, source_target_pairs={{0,1},{1,2},{2,3},{3,4},{4,5},{5,6},{6,7},{7,0},{8,9},{9,10},{10,1... | collective-permute-start | bytes 3080 | tf_op jit(solution)/shard_map/ppermute | solution.py:29
  337.1 4.5 %collective-permute-start.54 = (f32[1,1,4,64]{3,2,1,0:T(4,128)S(1)}, f32[1,1,4,64]{3,2,1,0:T(4,128)S(1)}, u32[]{:S(2)}, u32[]{:S(2)}) collective-permute-start(f32[1,1,4,64]{3,2,1,0:T(4,128)S(1)} %get-tuple-element.37), channel_id=1, source_target_pairs={{1,0},{2,1},{3,2},{4,3},{5,4},{6,5},{7,6},{0,7},{9,8},{10,9},{11,1... | collective-permute-start | bytes 3080 | tf_op jit(solution)/shard_map/ppermute | solution.py:31
  351.4 6.5 %collective-permute-start.59 = (f32[1,2,4,64]{3,2,1,0:T(4,128)S(1)}, f32[1,2,4,64]{3,2,1,0:T(4,128)S(1)}, u32[]{:S(2)}, u32[]{:S(2)}) collective-permute-start(f32[1,2,4,64]{3,2,1,0:T(4,128)S(1)} %get-tuple-element.30), channel_id=1, source_target_pairs={{0,8},{8,16},{16,24},{24,0},{1,9},{9,17},{17,25},{25,1},{2,10},{10... | collective-permute-start | bytes 6152 | tf_op jit(solution)/shard_map/ppermute | solution.py:29
  351.4 8.0 %collective-permute-start.60 = (f32[1,2,4,64]{3,2,1,0:T(4,128)S(1)}, f32[1,2,4,64]{3,2,1,0:T(4,128)S(1)}, u32[]{:S(2)}, u32[]{:S(2)}) collective-permute-start(f32[1,2,4,64]{3,2,1,0:T(4,128)S(1)} %get-tuple-element.30), channel_id=1, source_target_pairs={{8,0},{16,8},{24,16},{0,24},{9,1},{17,9},{25,17},{1,25},{10,2},{18... | collective-permute-start | bytes 6152 | tf_op jit(solution)/shard_map/ppermute | solution.py:31
  353.2 6.3 %collective-permute-start.57 = (f32[1,1,4,64]{3,2,1,0:T(4,128)S(1)}, f32[1,1,4,64]{3,2,1,0:T(4,128)S(1)}, u32[]{:S(2)}, u32[]{:S(2)}) collective-permute-start(f32[1,1,4,64]{3,2,1,0:T(4,128)S(1)} %get-tuple-element.32), channel_id=1, source_target_pairs={{0,1},{1,2},{2,3},{3,4},{4,5},{5,6},{6,7},{7,0},{8,9},{9,10},{10,1... | collective-permute-start | bytes 3080 | tf_op jit(solution)/shard_map/ppermute | solution.py:29
  354.5 4.9 %collective-permute-start.58 = (f32[1,1,4,64]{3,2,1,0:T(4,128)S(1)}, f32[1,1,4,64]{3,2,1,0:T(4,128)S(1)}, u32[]{:S(2)}, u32[]{:S(2)}) collective-permute-start(f32[1,1,4,64]{3,2,1,0:T(4,128)S(1)} %get-tuple-element.33), channel_id=1, source_target_pairs={{1,0},{2,1},{3,2},{4,3},{5,4},{6,5},{7,6},{0,7},{9,8},{10,9},{11,1... | collective-permute-start | bytes 3080 | tf_op jit(solution)/shard_map/ppermute | solution.py:31
  369.4 6.0 %collective-permute-start.61 = (f32[2,4]{0,1:T(4,128)S(1)}, f32[2,4]{0,1:T(4,128)S(1)}, u32[]{:S(2)}, u32[]{:S(2)}) collective-permute-start(f32[2,4]{0,1:T(4,128)S(1)} %bitcast.210), channel_id=1, source_target_pairs={{0,7},{1,0},{2,1},{3,2},{4,3},{5,4},{6,5},{7,6},{8,15},{9,8},{10,9... | collective-permute-start | bytes 104 | tf_op jit(solution)/shard_map/ppermute | solution.py:15
  379.2 4.5 %collective-permute-start.63 = (f32[8,4]{0,1:T(4,128)S(1)}, f32[8,4]{0,1:T(4,128)S(1)}, u32[]{:S(2)}, u32[]{:S(2)}) collective-permute-start(f32[8,4]{0,1:T(4,128)S(1)} %pad_maximum_fusion.21), channel_id=1, source_target_pairs={{0,4},{1,5},{2,6},{3,7},{4,0},{5,1},{6,2},{7,3},{8,12},{9,13},{10,... | collective-permute-start | bytes 392 | tf_op jit(solution)/shard_map/ppermute | solution.py:15
  384.3 8.5 %collective-permute-start.66 = (f32[1,2,4,64]{3,2,1,0:T(4,128)S(1)}, f32[1,2,4,64]{3,2,1,0:T(4,128)S(1)}, u32[]{:S(2)}, u32[]{:S(2)}) collective-permute-start(f32[1,2,4,64]{3,2,1,0:T(4,128)S(1)} %get-tuple-element.26), channel_id=1, source_target_pairs={{0,8},{8,16},{16,24},{24,0},{1,9},{9,17},{17,25},{25,1},{2,10},{10... | collective-permute-start | bytes 6152 | tf_op jit(solution)/shard_map/ppermute | solution.py:29
  384.3 10.1 %collective-permute-start.67 = (f32[1,2,4,64]{3,2,1,0:T(4,128)S(1)}, f32[1,2,4,64]{3,2,1,0:T(4,128)S(1)}, u32[]{:S(2)}, u32[]{:S(2)}) collective-permute-start(f32[1,2,4,64]{3,2,1,0:T(4,128)S(1)} %get-tuple-element.26), channel_id=1, source_target_pairs={{8,0},{16,8},{24,16},{0,24},{9,1},{17,9},{25,17},{1,25},{10,2},{18... | collective-permute-start | bytes 6152 | tf_op jit(solution)/shard_map/ppermute | solution.py:31
  386.1 8.3 %collective-permute-start.64 = (f32[1,1,4,64]{3,2,1,0:T(4,128)S(1)}, f32[1,1,4,64]{3,2,1,0:T(4,128)S(1)}, u32[]{:S(2)}, u32[]{:S(2)}) collective-permute-start(f32[1,1,4,64]{3,2,1,0:T(4,128)S(1)} %get-tuple-element.28), channel_id=1, source_target_pairs={{0,1},{1,2},{2,3},{3,4},{4,5},{5,6},{6,7},{7,0},{8,9},{9,10},{10,1... | collective-permute-start | bytes 3080 | tf_op jit(solution)/shard_map/ppermute | solution.py:29
  389.4 5.1 %collective-permute-start.65 = (f32[1,1,4,64]{3,2,1,0:T(4,128)S(1)}, f32[1,1,4,64]{3,2,1,0:T(4,128)S(1)}, u32[]{:S(2)}, u32[]{:S(2)}) collective-permute-start(f32[1,1,4,64]{3,2,1,0:T(4,128)S(1)} %get-tuple-element.29), channel_id=1, source_target_pairs={{1,0},{2,1},{3,2},{4,3},{5,4},{6,5},{7,6},{0,7},{9,8},{10,9},{11,1... | collective-permute-start | bytes 3080 | tf_op jit(solution)/shard_map/ppermute | solution.py:31
  (10 other events, 71.0 us)
